TPU v7x, 32 devices: a 4x4x1 block of a 4x4x8 slice. The times are simulated.
32 devices in a mesh: dp: 1 (over z), tp: 4 (over y), cp: 8 (over x, core).
Axes of the slice: x: 4, y: 4, z: 1, core: 2. Of those that a mesh axis runs over, the one named last changes fastest.
The devices are a block of a 4x4x8 slice.
Arguments:
- hidden_in: bfloat16 [512, 5120], P(('dp', 'cp', 'tp'))
- positions: int32 [512], P(('dp', 'cp', 'tp'))
- cache_len: int32 [1], P('dp')
- cache_k: bfloat16 [32768, 1024], P(('dp', 'cp', 'tp'))
- cache_v: bfloat16 [32768, 1024], P(('dp', 'cp', 'tp'))
- norm1_gain: bfloat16 [5120], replicated
- w_query: bfloat16 [5120, 4096], P(None, 'tp')
- w_key: bfloat16 [5120, 1024], P(None, 'tp')
- w_value: bfloat16 [5120, 1024], P(None, 'tp')
- w_out: bfloat16 [4096, 5120], P('tp')
- norm2_gain: bfloat16 [5120], replicated
- w_gate: bfloat16 [5120, 14336], P(None, 'tp')
- w_up: bfloat16 [5120, 14336], P(None, 'tp')
- w_down: bfloat16 [14336, 5120], P('tp')
Outputs:
- output: bfloat16 [512, 5120], P(('dp', 'cp', 'tp'))
All inputs are finite; a program needn't handle non-finite values.
Results may differ from a plain program's by a relative error of at most 0.00935577.
Values are sent between devices in bfloat16 or wider.
A program may use at most 768 MiB of HBM per device.

v0:
```python
import math
import jax
import jax.numpy as jnp
from jax import lax
from jax.sharding import PartitionSpec as P

HEAD_DIM = 128
ROPE_BASE = 500000.0
NORM_EPS = 1e-5


def rms_norm(hidden, norm_gain):
    values = hidden.astype(jnp.float32)
    inv_rms = lax.rsqrt(jnp.mean(values * values, axis=-1, keepdims=True) + NORM_EPS)
    return (values * inv_rms * norm_gain.astype(jnp.float32)).astype(jnp.bfloat16)


def rotary(projected, positions):
    half_dim = HEAD_DIM // 2
    inv_freq = 1.0 / (ROPE_BASE ** (jnp.arange(half_dim, dtype=jnp.float32) * (2.0 / HEAD_DIM)))
    angles = positions.astype(jnp.float32)[:, None] * inv_freq[None, :]
    expand = (angles.shape[0],) + (1,) * (projected.ndim - 2) + (half_dim,)
    cos_table = jnp.cos(angles).reshape(expand)
    sin_table = jnp.sin(angles).reshape(expand)
    first_half = projected[..., :half_dim]
    second_half = projected[..., half_dim:]
    rotated = jnp.concatenate([first_half * cos_table - second_half * sin_table, second_half * cos_table + first_half * sin_table], axis=-1)
    return rotated.astype(jnp.bfloat16)


def attend_rows(block_queries, block_pos, cache_keys, cache_values, cache_valid, new_keys, new_values, all_pos):
    score_scale = 1.0 / math.sqrt(HEAD_DIM)
    cache_scores = jnp.einsum('rkgd,skd->krgs', block_queries, cache_keys, preferred_element_type=jnp.float32) * score_scale
    new_scores = jnp.einsum('rkgd,skd->krgs', block_queries, new_keys, preferred_element_type=jnp.float32) * score_scale
    cache_scores = jnp.where(cache_valid, cache_scores, -jnp.inf)
    causal = all_pos[None, None, None, :] <= block_pos[None, :, None, None]
    new_scores = jnp.where(causal, new_scores, -jnp.inf)
    row_max = jnp.maximum(jnp.max(cache_scores, axis=-1, keepdims=True), jnp.max(new_scores, axis=-1, keepdims=True))
    cache_probs = jnp.exp(cache_scores - row_max)
    new_probs = jnp.exp(new_scores - row_max)
    normalizer = jnp.sum(cache_probs, axis=-1, keepdims=True) + jnp.sum(new_probs, axis=-1, keepdims=True)
    weighted = jnp.einsum('krgs,skd->krgd', cache_probs.astype(jnp.bfloat16), cache_values, preferred_element_type=jnp.float32)
    weighted = weighted + jnp.einsum('krgs,skd->krgd', new_probs.astype(jnp.bfloat16), new_values, preferred_element_type=jnp.float32)
    return jnp.transpose((weighted / normalizer).astype(jnp.bfloat16), (1, 0, 2, 3))


def solution(mesh):
    tp_size = mesh.shape['tp']
    token_spec = P(('dp', 'cp', 'tp'), None)
    column_spec = P(None, 'tp')
    row_spec = P('tp', None)

    def device_layer(hidden_loc, pos_loc, cache_len, cache_k, cache_v, norm1_gain, w_query, w_key, w_value, w_out, norm2_gain, w_gate, w_up, w_down):
        shard_rows = hidden_loc.shape[0]
        kv_local = w_key.shape[1] // HEAD_DIM
        groups = w_query.shape[1] // w_key.shape[1]
        normed = rms_norm(hidden_loc, norm1_gain)
        group_in = lax.all_gather(normed, 'tp', axis=0, tiled=True)
        group_pos = lax.all_gather(pos_loc, 'tp', axis=0, tiled=True)
        group_rows = group_in.shape[0]
        queries = rotary(jnp.dot(group_in, w_query, preferred_element_type=jnp.float32).reshape(group_rows, kv_local, groups, HEAD_DIM), group_pos)
        keys_loc = rotary(jnp.dot(group_in, w_key, preferred_element_type=jnp.float32).reshape(group_rows, kv_local, HEAD_DIM), group_pos)
        values_loc = jnp.dot(group_in, w_value, preferred_element_type=jnp.float32).astype(jnp.bfloat16).reshape(group_rows, kv_local, HEAD_DIM)
        new_keys = lax.all_gather(keys_loc, 'cp', axis=0, tiled=True)
        new_values = lax.all_gather(values_loc, 'cp', axis=0, tiled=True)
        all_pos = lax.all_gather(group_pos, 'cp', axis=0, tiled=True)
        cache_keys = lax.all_gather(lax.all_to_all(cache_k, 'tp', 1, 0, tiled=True), 'cp', axis=0, tiled=True).reshape(-1, kv_local, HEAD_DIM)
        cache_values = lax.all_gather(lax.all_to_all(cache_v, 'tp', 1, 0, tiled=True), 'cp', axis=0, tiled=True).reshape(-1, kv_local, HEAD_DIM)
        cache_valid = jnp.arange(cache_keys.shape[0]) < cache_len[0]
        block_queries = queries.reshape(tp_size, shard_rows, kv_local, groups, HEAD_DIM)
        block_pos = group_pos.reshape(tp_size, shard_rows)

        def attend_block(block_item):
            return attend_rows(block_item[0], block_item[1], cache_keys, cache_values, cache_valid, new_keys, new_values, all_pos)

        attended = lax.map(attend_block, (block_queries, block_pos)).reshape(group_rows, kv_local * groups * HEAD_DIM)
        attn_part = jnp.dot(attended, w_out, preferred_element_type=jnp.float32)
        residual_mid = (hidden_loc.astype(jnp.float32) + lax.psum_scatter(attn_part, 'tp', scatter_dimension=0, tiled=True)).astype(jnp.bfloat16)
        group_mid = lax.all_gather(rms_norm(residual_mid, norm2_gain), 'tp', axis=0, tiled=True)
        gate_proj = jnp.dot(group_mid, w_gate, preferred_element_type=jnp.float32)
        up_proj = jnp.dot(group_mid, w_up, preferred_element_type=jnp.float32)
        hidden_mlp = (jax.nn.silu(gate_proj) * up_proj).astype(jnp.bfloat16)
        mlp_part = jnp.dot(hidden_mlp, w_down, preferred_element_type=jnp.float32)
        return (residual_mid.astype(jnp.float32) + lax.psum_scatter(mlp_part, 'tp', scatter_dimension=0, tiled=True)).astype(jnp.bfloat16)

    return jax.shard_map(device_layer, mesh=mesh, in_specs=(token_spec, P(('dp', 'cp', 'tp')), P('dp'), token_spec, token_spec, P(), column_spec, column_spec, column_spec, row_spec, P(), column_spec, column_spec, row_spec), out_specs=token_spec, check_vma=False)
```

profile of v0, /device:TPU:99, one launch (start us, length us, event | category | flops | bytes accessed | tf_op | source)
XLA Modules:
  0.0 514.5 jit_solution(16303094105966819229)
XLA Ops:
  10.7 31.3 %all_to_all.38 = bf16[1024,4,256]{0,2,1:T(8,128)(2,1)} all-to-all(bf16[1024,4,256]{0,2,1:T(8,128)(2,1)} %bitcast.106), channel_id=1, replica_groups=mesh['dp'=1,'tp'=4,'cp'=8] {'tp'}, dimensions={1} | all-to-all | bytes 4194304 | tf_op jit(solution)/shard_map/all_to_all | solution.py:67
  50.0 29.1 %all_to_all.39 = bf16[1024,4,256]{0,2,1:T(8,128)(2,1)} all-to-all(bf16[1024,4,256]{0,2,1:T(8,128)(2,1)} %bitcast.107), channel_id=1, replica_groups=mesh['dp'=1,'tp'=4,'cp'=8] {'tp'}, dimensions={1} | all-to-all | bytes 4194304 | tf_op jit(solution)/shard_map/all_to_all | solution.py:68
  90.3 10.6 %all_gather.24 = bf16[64,5120]{1,0:T(8,128)(2,1)S(1)} all-gather(bf16[16,5120]{1,0:T(8,128)(2,1)S(1)} %fusion.39), channel_id=1, replica_groups=mesh['dp'=1,'tp'=4,'cp'=8] {'tp'}, dimensions={0}, use_global_device_ids=true | all-gather | bytes 819200 | tf_op jit(solution)/shard_map/all_gather | solution.py:58
  112.0 13.4 %all-reduce.1 = s32[512]{0:T(512)S(1)} all-reduce(s32[512]{0:T(512)S(1)} %dynamic-update-slice.1), channel_id=1, replica_groups=mesh['dp'=1,'tp'=4,'cp'=8] {'cp'}, use_global_device_ids=true, to_apply=%add.1 | all-reduce | flops 512 | bytes 4096
  126.8 18.4 %all_gather.28 = bf16[512,2,128]{2,0,1:T(8,128)(2,1)S(1)} all-gather(bf16[64,2,128]{2,0,1:T(8,128)(2,1)S(1)} %pad_maximum_fusion.1), channel_id=1, replica_groups=mesh['dp'=1,'tp'=4,'cp'=8] {'cp'}, dimensions={0}, use_global_device_ids=true | all-gather | bytes 294912 | tf_op jit(solution)/shard_map/all_gather | solution.py:64
  145.1 25.2 %all_gather.30 = bf16[512,2,128]{2,0,1:T(8,128)(2,1)S(1)} all-gather(bf16[64,2,128]{2,0,1:T(8,128)(2,1)S(1)} %bitcast.110), channel_id=1, replica_groups=mesh['dp'=1,'tp'=4,'cp'=8] {'cp'}, dimensions={0}, use_global_device_ids=true | all-gather | bytes 294912 | tf_op jit(solution)/shard_map/all_gather | solution.py:65
  170.8 21.3 %copy.33 = bf16[32768,256]{0,1:T(8,128)(2,1)} copy(bf16[32768,256]{1,0:T(8,128)(2,1)} %all-gather.3.cloned.1.call-done) | data formatting | bytes 33554432 | tf_op jit(solution)/shard_map/all_gather | solution.py:67
  192.1 21.2 %copy.41 = bf16[32768,2,128]{2,0,1:T(8,128)(2,1)} copy(bf16[32768,2,128]{0,2,1:T(8,128)(2,1)} %bitcast.100) | data formatting | bytes 33554432
  216.1 21.2 %copy.38 = bf16[32768,256]{0,1:T(8,128)(2,1)} copy(bf16[32768,256]{1,0:T(8,128)(2,1)} %all-gather.5.cloned.1.call-done) | data formatting | bytes 33554432 | tf_op jit(solution)/shard_map/all_gather | solution.py:68
  237.4 21.2 %copy.42 = bf16[32768,2,128]{2,0,1:T(8,128)(2,1)} copy(bf16[32768,2,128]{0,2,1:T(8,128)(2,1)} %bitcast.101) | data formatting | bytes 33554432
  258.6 139.7 %while.11 = (s32[]{:T(128)}, bf16[4,16,2,4,128]{4,3,2,1,0:T(4,128)(2,1)S(1)}, bf16[4,16,2,4,128]{4,1,0,3,2:T(8,128)(2,1)S(1)}, bf16[32768,2,128]{2,0,1:T(8,128)(...) while((s32[]{:T(128)}, ...), condition=%wide.region_6.7_spmd.clone, body=%wide.region_1.6_spmd.clone.sunk | while | flops 2210947072 | bytes 85583680 | solution.py:76
  259.7 12.7 %fusion.83 = (f32[2,16,4]{1,2,0:T(4,128)S(1)}, f32[2,16,4,32768]{3,1,2,0:T(8,128)}) fusion(bf16[32768,2,128]{2,0,1:T(8,128)(2,1)} %get-tuple-element.231, bf16[4,16,2,4,128]{4,1,0,3,2:T(8,128)(2,1)S(1)} %get-tuple-element.230, s32[]{:T(128)} %get-tuple-element.217, pred[32768]{0:T(1024)(128)(4,1)S(1)} %iota_compare_fusion.2), kind=kOutput, calls=%fused_computation.73.clone.1 | convolution fusion | flops 1086324608 | bytes 33620484 | tf_op jit(solution)/shard_map/while/body/eval_jaxpr/rkgd,skd->krgs/dot_general | solution.py:33
  280.8 12.4 %fusion.86 = f32[2,16,4,128]{3,1,2,0:T(8,128)S(1)} fusion(bf16[32768,2,128]{2,0,1:T(8,128)(2,1)} %get-tuple-element.235, f32[2,16,4,32768]{3,1,2,0:T(8,128)} %get-tuple-element.202, f32[2,16,4]{1,2,0:T(4,128)S(1)} %max.10), kind=kOutput, calls=%fused_computation.3.clone.1 | convolution fusion | flops 1082130432 | bytes 33620480 | tf_op jit(solution)/shard_map/while/body/eval_jaxpr/krgs,skd->krgd/dot_general | solution.py:42
  294.6 12.7 %fusion.83 = (f32[2,16,4]{1,2,0:T(4,128)S(1)}, f32[2,16,4,32768]{3,1,2,0:T(8,128)}) fusion(bf16[32768,2,128]{2,0,1:T(8,128)(2,1)} %get-tuple-element.231, bf16[4,16,2,4,128]{4,1,0,3,2:T(8,128)(2,1)S(1)} %get-tuple-element.230, s32[]{:T(128)} %get-tuple-element.217, pred[32768]{0:T(1024)(128)(4,1)S(1)} %iota_compare_fusion.2), kind=kOutput, calls=%fused_computation.73.clone.1 | convolution fusion | flops 1086324608 | bytes 33620484 | tf_op jit(solution)/shard_map/while/body/eval_jaxpr/rkgd,skd->krgs/dot_general | solution.py:33
  315.7 12.4 %fusion.86 = f32[2,16,4,128]{3,1,2,0:T(8,128)S(1)} fusion(bf16[32768,2,128]{2,0,1:T(8,128)(2,1)} %get-tuple-element.235, f32[2,16,4,32768]{3,1,2,0:T(8,128)} %get-tuple-element.202, f32[2,16,4]{1,2,0:T(4,128)S(1)} %max.10), kind=kOutput, calls=%fused_computation.3.clone.1 | convolution fusion | flops 1082130432 | bytes 33620480 | tf_op jit(solution)/shard_map/while/body/eval_jaxpr/krgs,skd->krgd/dot_general | solution.py:42
  329.5 12.7 %fusion.83 = (f32[2,16,4]{1,2,0:T(4,128)S(1)}, f32[2,16,4,32768]{3,1,2,0:T(8,128)}) fusion(bf16[32768,2,128]{2,0,1:T(8,128)(2,1)} %get-tuple-element.231, bf16[4,16,2,4,128]{4,1,0,3,2:T(8,128)(2,1)S(1)} %get-tuple-element.230, s32[]{:T(128)} %get-tuple-element.217, pred[32768]{0:T(1024)(128)(4,1)S(1)} %iota_compare_fusion.2), kind=kOutput, calls=%fused_computation.73.clone.1 | convolution fusion | flops 1086324608 | bytes 33620484 | tf_op jit(solution)/shard_map/while/body/eval_jaxpr/rkgd,skd->krgs/dot_general | solution.py:33
  350.6 12.4 %fusion.86 = f32[2,16,4,128]{3,1,2,0:T(8,128)S(1)} fusion(bf16[32768,2,128]{2,0,1:T(8,128)(2,1)} %get-tuple-element.235, f32[2,16,4,32768]{3,1,2,0:T(8,128)} %get-tuple-element.202, f32[2,16,4]{1,2,0:T(4,128)S(1)} %max.10), kind=kOutput, calls=%fused_computation.3.clone.1 | convolution fusion | flops 1082130432 | bytes 33620480 | tf_op jit(solution)/shard_map/while/body/eval_jaxpr/krgs,skd->krgd/dot_general | solution.py:42
  364.4 12.7 %fusion.83 = (f32[2,16,4]{1,2,0:T(4,128)S(1)}, f32[2,16,4,32768]{3,1,2,0:T(8,128)}) fusion(bf16[32768,2,128]{2,0,1:T(8,128)(2,1)} %get-tuple-element.231, bf16[4,16,2,4,128]{4,1,0,3,2:T(8,128)(2,1)S(1)} %get-tuple-element.230, s32[]{:T(128)} %get-tuple-element.217, pred[32768]{0:T(1024)(128)(4,1)S(1)} %iota_compare_fusion.2), kind=kOutput, calls=%fused_computation.73.clone.1 | convolution fusion | flops 1086324608 | bytes 33620484 | tf_op jit(solution)/shard_map/while/body/eval_jaxpr/rkgd,skd->krgs/dot_general | solution.py:33
  385.6 12.4 %fusion.86 = f32[2,16,4,128]{3,1,2,0:T(8,128)S(1)} fusion(bf16[32768,2,128]{2,0,1:T(8,128)(2,1)} %get-tuple-element.235, f32[2,16,4,32768]{3,1,2,0:T(8,128)} %get-tuple-element.202, f32[2,16,4]{1,2,0:T(4,128)S(1)} %max.10), kind=kOutput, calls=%fused_computation.3.clone.1 | convolution fusion | flops 1082130432 | bytes 33620480 | tf_op jit(solution)/shard_map/while/body/eval_jaxpr/krgs,skd->krgd/dot_general | solution.py:42
  405.5 21.0 %reduce-scatter.3.cloned.1.call-done = f32[16,5120]{1,0:T(8,128)} async-done(((f32[64,5120]{1,0:T(8,128)}), f32[16,5120]{1,0:T(8,128)}) %reduce-scatter.3.cloned.1.call-update) | async-done | bytes 327696 | tf_op jit(solution)/shard_map/reduce_scatter | solution.py:78
  427.8 11.9 %all_gather.31 = bf16[64,5120]{1,0:T(8,128)(2,1)S(1)} all-gather(bf16[16,5120]{1,0:T(8,128)(2,1)S(1)} %fusion.43), channel_id=1, replica_groups=mesh['dp'=1,'tp'=4,'cp'=8] {'tp'}, dimensions={0}, use_global_device_ids=true | all-gather | bytes 819200 | tf_op jit(solution)/shard_map/all_gather | solution.py:79
  439.7 15.6 %fusion.54 = f32[64,3584]{1,0:T(8,128)} fusion(bf16[64,5120]{1,0:T(8,128)(2,1)S(1)} %all_gather.31, bf16[5120,3584]{1,0:T(8,128)(2,1)} %param.27), kind=kOutput, calls=%fused_computation.80 | convolution fusion | flops 2348810240 | bytes 38273024 | tf_op jit(solution)/shard_map/dot_general | solution.py:80
  455.3 26.9 %fusion.29 = f32[64,5120]{1,0:T(8,128)} fusion(bf16[3584,5120]{1,0:T(8,128)(2,1)} %param.29, bf16[64,5120]{1,0:T(8,128)(2,1)S(1)} %all_gather.31, bf16[5120,3584]{1,0:T(8,128)(2,1)} %param.28, f32[64,3584]{1,0:T(8,128)} %fusion.54), kind=kOutput, calls=%fused_computation.37 | convolution fusion | flops 4698996736 | bytes 76283904 | tf_op jit(solution)/shard_map/dot_general | solution.py:83
  482.3 24.0 %reduce-scatter.5.cloned.1.call-done = f32[16,5120]{1,0:T(8,128)} async-done(((f32[64,5120]{1,0:T(8,128)}), f32[16,5120]{1,0:T(8,128)}) %reduce-scatter.5.cloned.1.call-update) | async-done | bytes 327696 | tf_op jit(solution)/shard_map/reduce_scatter | solution.py:84
  (111 shorter events, 86.8 us)
Async XLA Ops:
  6.5 94.3 %copy-start = (bf16[5120,256]{1,0:T(8,128)(2,1)S(1)}, bf16[5120,256]{1,0:T(8,128)(2,1)}, u32[]{:S(2)}) copy-start(bf16[5120,256]{1,0:T(8,128)(2,1)} %param.23) | copy-start | bytes 7864324
  6.6 76.6 %copy-start.10 = (u32[32]{0:T(128)S(1)}, u32[32]{0:T(128)}, u32[]{:S(2)}) copy-start(u32[32]{0:T(128)} %constant.42) | copy-start | bytes 388
  6.6 77.9 %copy-start.8 = (s32[16]{0:T(128)S(1)}, s32[16]{0:T(128)}, u32[]{:S(2)}) copy-start(s32[16]{0:T(128)} %param.17) | copy-start | bytes 196
  6.6 83.4 %copy-start.6 = (bf16[5120]{0:T(1024)(128)(2,1)S(1)}, bf16[5120]{0:T(1024)(128)(2,1)}, u32[]{:S(2)}) copy-start(bf16[5120]{0:T(1024)(128)(2,1)} %param.21) | copy-start | bytes 30724
  6.6 83.4 %copy-start.3 = (bf16[16,5120]{1,0:T(8,128)(2,1)S(1)}, bf16[16,5120]{1,0:T(8,128)(2,1)}, u32[]{:S(2)}) copy-start(bf16[16,5120]{1,0:T(8,128)(2,1)} %param.16) | copy-start | bytes 491524
  6.6 164.3 %all-gather.3.cloned.1.call-start = ((), (), s32[]{:S(2)}) async-start(), calls=%async_computation.4 | async-start | bytes 18874368 | tf_op jit(solution)/shard_map/all_gather | solution.py:67
  46.0 170.1 %all-gather.5.cloned.1.call-start = ((), (), s32[]{:S(2)}) async-start(), calls=%async_computation.5 | async-start | bytes 18874368 | tf_op jit(solution)/shard_map/all_gather | solution.py:68
  50.0 59.9 %copy-start.9 = (u32[32]{0:T(128)S(1)}, u32[32]{0:T(128)}, u32[]{:S(2)}) copy-start(u32[32]{0:T(128)} %constant.47) | copy-start | bytes 388
  83.1 343.4 %reduce-scatter.3.cloned.1.call-start = ((), (), s32[]{:S(2)}) async-start(), calls=%async_computation.6 | async-start | bytes 1638400 | tf_op jit(solution)/shard_map/reduce_scatter | solution.py:78
  101.4 9.1 %copy-start.2 = (bf16[5120,256]{1,0:T(8,128)(2,1)S(1)}, bf16[5120,256]{1,0:T(8,128)(2,1)}, u32[]{:S(2)}) copy-start(bf16[5120,256]{1,0:T(8,128)(2,1)} %param.24) | copy-start | bytes 7864324
  237.4 21.2 %copy-start.5 = (bf16[4,16,2,4,128]{4,3,2,1,0:T(4,128)(2,1)S(1)}, bf16[4,16,2,4,128]{4,3,2,1,0:T(4,128)(2,1)}, u32[]{:S(2)}) copy-start(bf16[4,16,2,4,128]{4,3,2,1,0:T(4,128)(2,1)} %custom-call) | copy-start | bytes 393220
  398.3 7.2 %copy-start.7 = (bf16[5120]{0:T(1024)(128)(2,1)S(1)}, bf16[5120]{0:T(1024)(128)(2,1)}, u32[]{:S(2)}) copy-start(bf16[5120]{0:T(1024)(128)(2,1)} %param.26) | copy-start | bytes 30724
  398.3 28.2 %copy-start.4 = (bf16[16,5120]{1,0:T(8,128)(2,1)S(1)}, bf16[16,5120]{1,0:T(8,128)(2,1)}, u32[]{:S(2)}) copy-start(bf16[16,5120]{1,0:T(8,128)(2,1)} %param.16) | copy-start | bytes 491524
  405.4 100.8 %reduce-scatter.5.cloned.1.call-start = ((), (), s32[]{:S(2)}) async-start(), calls=%async_computation.7 | async-start | bytes 1638400 | tf_op jit(solution)/shard_map/reduce_scatter | solution.py:84
  455.3 52.6 %copy-start.1 = (bf16[5120,256]{1,0:T(8,128)(2,1)S(1)}, bf16[5120,256]{1,0:T(8,128)(2,1)}, u32[]{:S(2)}) copy-start(bf16[5120,256]{1,0:T(8,128)(2,1)} %param.23) | copy-start | bytes 7864324
Sparse Core Ops, SparseCore 0:
  46.1 83.1 all-gather.2
  130.9 85.1 all-gather.4
  405.6 20.9 reduce-scatter.2
  482.4 23.8 reduce-scatter.4
where the time goes:
time: 520 us; the launch traced here: 514 us
  matrix products  160 us (31%)
  blocking collectives  145 us (28%)
  local copies, waits for them, and re-layouts  106 us (20%)
  waiting for transfers between devices  48.1 us (9%)
  other arithmetic  40.4 us (8%)
  between operations  14.7 us (3%)
    unnamed x32, local copies, waits for them, and re-layouts  52.2 us
    dot_general x4, matrix products, attend_rows(): jnp.einsum('rkgd,skd->krgs', block_queries, cache_keys, preferred_element...  50.8 us
    dot_general x4, matrix products, attend_rows(): jnp.einsum('krgs,skd->krgd', cache_probs.astype(jnp.bfloat16), cache_valu...  49.7 us
    reduce_sum x4, other arithmetic, attend_rows(): jnp.sum(cache_probs, axis=-1, keepdims=True)  32.9 us
    all_to_all x1, blocking collectives, device_layer(): lax.all_to_all(cache_k, 'tp', 1, 0, tiled=True)  31.3 us
    all_to_all x1, blocking collectives, device_layer(): lax.all_to_all(cache_v, 'tp', 1, 0, tiled=True)  29.1 us
    dot_general x1, matrix products, device_layer(): mlp_part = jnp.dot(hidden_mlp, w_down, preferred_element_type=jnp.float32)  26.9 us
    all_gather x1, blocking collectives, device_layer(): new_values = lax.all_gather(values_loc, 'cp', axis=0, tiled=True)  25.2 us
  transfers between devices with their start and end apart: 4, of which 3 were waited for; matrix products, arithmetic and copies ran while one was open for 12% of the time, Pallas kernels for 0%

commit v1 on v0

v1 whole, which is shorter than its diff:
```python
import functools
import math
import jax
import jax.numpy as jnp
from jax import lax
from jax.experimental import pallas as pl
from jax.experimental.pallas import tpu as pltpu
from jax.sharding import PartitionSpec as P

HEAD_DIM = 128
ROPE_BASE = 500000.0
NORM_EPS = 1e-5
MESH = pl.DeviceIdType.MESH
F32 = jnp.float32
BF16 = jnp.bfloat16
M_INIT = -3e38
EXP_SCALE = math.log2(math.e) / math.sqrt(HEAD_DIM)
RING = 4
ANY = pl.BlockSpec(memory_space=pl.ANY)
VMEM = pl.BlockSpec(memory_space=pltpu.VMEM)
SMEM = pl.BlockSpec(memory_space=pltpu.SMEM)


class Place:
    def __init__(self):
        self.y = lax.axis_index('tp')
        cp = lax.axis_index('cp')
        self.x = cp // 2
        self.core = cp % 2

    def at(self, dx=0, dy=0, other=False):
        core = 1 - self.core if other else self.core
        return {'tp': (self.y + dy) % RING, 'cp': ((self.x + dx) % RING) * 2 + core}


def remote(src, dst, send_sem, recv_sem, device):
    return pltpu.make_async_remote_copy(src_ref=src, dst_ref=dst, send_sem=send_sem, recv_sem=recv_sem, device_id=device, device_id_type=MESH)


def barrier(devices):
    sem = pltpu.get_barrier_semaphore()
    for device in devices:
        pl.semaphore_signal(sem, inc=1, device_id=device, device_id_type=MESH)
    pl.semaphore_wait(sem, len(devices))


def ring_gather(pos, right, left, block, half, sends, recvs, own=None, partner=None, core=None, psends=None, precvs=None, between=None):
    prev, nxt, far = (pos + 3) % RING, (pos + 1) % RING, (pos + 2) % RING
    mine = block(pos, core) if own is None else own
    to_right = remote(mine, block(pos, core), sends.at[0], recvs.at[0], right)
    to_left = remote(mine, block(pos, core), sends.at[1], recvs.at[1], left)
    to_right.start()
    to_left.start()
    copies = [to_right, to_left]
    given = []

    def give(p, i, source=None):
        if partner is not None:
            copy = remote(block(p, core) if source is None else source, block(p, core), psends.at[i], precvs.at[i], partner)
            copy.start()
            given.append(copy)

    give(pos, 0, mine)
    remote(block(prev, core), block(prev, core), sends.at[0], recvs.at[0], left).wait_recv()
    fwd_right = remote(half(prev, core, 0), half(prev, core, 0), sends.at[2], recvs.at[2], right)
    fwd_right.start()
    give(prev, 1)
    remote(block(nxt, core), block(nxt, core), sends.at[1], recvs.at[1], right).wait_recv()
    fwd_left = remote(half(nxt, core, 1), half(nxt, core, 1), sends.at[3], recvs.at[3], left)
    fwd_left.start()
    give(nxt, 2)
    copies += [fwd_right, fwd_left]
    if between is not None:
        between()
    remote(half(far, core, 0), half(far, core, 0), sends.at[2], recvs.at[2], left).wait_recv()
    remote(half(far, core, 1), half(far, core, 1), sends.at[3], recvs.at[3], right).wait_recv()
    give(far, 3)
    if partner is not None:
        for i, p in enumerate((pos, prev, nxt, far)):
            remote(block(p, 1 - core), block(p, 1 - core), psends.at[i], precvs.at[i], partner).wait_recv()
    return copies + given


def attention_kernel(x_in, len_ref, ck, cv, gain, wq, wk, wv, cos_ref, sin_ref, relq_ref, relk_ref, o_out, xres_out,
                     xbuf, abuf, wqv, wkv, wvv, kbuf, vbuf, vt, qall, knew, vnew, acc, r1l, r1r, r2l, r2r, obuf,
                     lsem, xs, xr, ps, pr, kvs, kvr, qs, qr, rs, rr, os, orr):
    me = Place()
    x, y, core = me.x, me.y, me.core
    width = x_in.shape[1]
    half_w = width // 2
    slots = ck.shape[0]
    rows = qall.shape[0]
    chip_rows = rows // RING
    heads = acc.shape[0]
    head_w = heads * HEAD_DIM
    col = [(dy, dk) for dy in (0, 1, 3, 2) for dk in (0, 1)]
    partner = me.at(other=True)
    up, down = me.at(dy=1), me.at(dy=-1 + RING)
    right, left = me.at(dx=1), me.at(dx=-1 + RING)

    local = [
        pltpu.make_async_copy(x_in, xbuf.at[y, core], lsem.at[0]),
        pltpu.make_async_copy(wq.at[:, pl.ds(pl.multiple_of(core * head_w, head_w), head_w)], wqv, lsem.at[1]),
        pltpu.make_async_copy(wk.at[:, pl.ds(pl.multiple_of(core * HEAD_DIM, HEAD_DIM), HEAD_DIM)], wkv, lsem.at[2]),
        pltpu.make_async_copy(wv.at[:, pl.ds(pl.multiple_of(core * HEAD_DIM, HEAD_DIM), HEAD_DIM)], wvv, lsem.at[3]),
    ]
    for copy in local:
        copy.start()

    barrier([me.at(dy=dy, other=bool(dk)) for dy, dk in col[1:]] + [right, left])

    kv_copies = []

    def send_kv():
        for s, (dy, dk) in enumerate(col):
            head = 2 * ((y + dy) % RING) + (1 - core if dk else core)
            lanes = pl.ds(pl.multiple_of(head * HEAD_DIM, HEAD_DIM), HEAD_DIM)
            for i, (src, dst) in enumerate(((ck, kbuf), (cv, vbuf))):
                if s == 0:
                    copy = pltpu.make_async_copy(src.at[:, lanes], dst.at[s], kvr.at[s, i])
                else:
                    copy = remote(src.at[:, lanes], dst.at[s], kvs.at[s, i], kvr.at[s, i], me.at(dy=dy, other=bool(dk)))
                    kv_copies.append(copy)
                copy.start()

    x_copies = ring_gather(
        y, up, down, lambda p, c: xbuf.at[p, c], lambda p, c, i: xbuf.at[p, c, :, pl.ds(i * half_w, half_w)],
        xs, xr, own=x_in, partner=partner, core=core, psends=ps, precvs=pr, between=send_kv)
    local[0].wait()

    def norm_block(i, carry):
        values = xbuf[i].reshape(2 * xbuf.shape[2], width).astype(F32)
        inv = lax.rsqrt(jnp.mean(values * values, axis=-1, keepdims=True) + NORM_EPS)
        abuf[i] = (values * inv * gain[...].astype(F32)).astype(BF16)
        return carry

    lax.fori_loop(0, RING, norm_block, 0)
    xres_out[...] = xbuf[y, :, :, pl.ds(pl.multiple_of(core * half_w, half_w), half_w)].reshape(xres_out.shape)

    for copy in local[1:]:
        copy.wait()
    normed = abuf[...].reshape(chip_rows, width)
    cos, sin = cos_ref[...], sin_ref[...]

    def rotate(v):
        return (v * cos + pltpu.roll(v, HEAD_DIM // 2, 1) * sin).astype(BF16)

    my_rows = pl.ds(pl.multiple_of(x * chip_rows, chip_rows), chip_rows)
    q = jnp.dot(normed, wqv[...], preferred_element_type=F32)
    for h in range(heads):
        qall[my_rows, h * HEAD_DIM:(h + 1) * HEAD_DIM] = rotate(q[:, h * HEAD_DIM:(h + 1) * HEAD_DIM])
    knew[...] = rotate(jnp.dot(normed, wkv[...], preferred_element_type=F32))
    vnew[...] = jnp.dot(normed, wvv[...], preferred_element_type=F32).astype(BF16)

    def q_rows(p):
        return pl.ds(pl.multiple_of(p * chip_rows, chip_rows), chip_rows)

    q_copies = ring_gather(
        x, right, left, lambda p, c: qall.at[q_rows(p), :],
        lambda p, c, i: qall.at[q_rows(p), pl.ds(i * head_w // 2, head_w // 2)], qs, qr)

    tile = 256
    tiles = rows // tile

    def softmax_step(keys, vt_value, h, j, mask_of, first):
        lanes = pl.ds(j * tile, tile)
        queries = qall[j * tile:(j + 1) * tile, pl.ds(pl.multiple_of(h * HEAD_DIM, HEAD_DIM), HEAD_DIM)]
        s = lax.dot_general(keys, queries, (((1,), (1,)), ((), ())), preferred_element_type=F32)
        s = jnp.where(mask_of(j, s.shape), s, -jnp.inf)
        top = jnp.max(s, axis=0, keepdims=True)
        if first:
            m_new = jnp.maximum(top, M_INIT)
        else:
            m_old = acc[h, HEAD_DIM:HEAD_DIM + 1, lanes]
            l_old = acc[h, HEAD_DIM + 1:HEAD_DIM + 2, lanes]
            m_new = jnp.maximum(top, m_old)
        e = jnp.exp2(s * EXP_SCALE - m_new * EXP_SCALE)
        l_new = jnp.sum(e, axis=0, keepdims=True)
        o = jnp.dot(vt_value, e.astype(BF16), preferred_element_type=F32)
        if not first:
            alpha = jnp.exp2((m_old - m_new) * EXP_SCALE)
            l_new = l_new + l_old * alpha
            o = o + acc[h, 0:HEAD_DIM, lanes] * alpha
        acc[h, 0:HEAD_DIM, lanes] = o
        acc[h, HEAD_DIM:HEAD_DIM + 1, lanes] = m_new
        acc[h, HEAD_DIM + 1:HEAD_DIM + 2, lanes] = l_new

    vnew_t = vnew[...].astype(F32).T.astype(BF16)
    relk = relk_ref[...]

    def new_head(h, carry):
        for j in range(tiles):
            softmax_step(knew[...], vnew_t, h, j, lambda j, shape: jnp.broadcast_to(relk, shape) <= jnp.broadcast_to(relq_ref[:, j * tile:(j + 1) * tile], shape), True)
        return carry

    lax.fori_loop(0, heads, new_head, 0)
    cache_len = len_ref[0]

    def source(s, carry):
        u, dk = s // 2, s % 2
        dy = u + (u // 2) * (1 - 2 * (u % 2))
        src_core = core + dk * (1 - 2 * core)
        src_y = (y - dy + RING) % RING
        base = ((2 * x + src_core) * RING + src_y) * slots
        for i, (src, dst) in enumerate(((ck, kbuf), (cv, vbuf))):
            pltpu.make_async_copy(src.at[:, pl.ds(0, HEAD_DIM)], dst.at[s], kvr.at[s, i]).wait()
        vt[...] = vbuf[s].astype(F32).T.astype(BF16)
        seen = cache_len - base

        def head(h, c):
            for j in range(tiles):
                softmax_step(kbuf[s], vt[...], h, j, lambda j, shape: lax.broadcasted_iota(jnp.int32, shape, 0) < seen, False)
            return c

        return lax.fori_loop(0, heads, head, carry)

    lax.fori_loop(0, len(col), source, 0)

    hh = heads // 2
    far, nxt, prev = (x + 2) % RING, (x + 1) % RING, (x + 3) % RING
    p1 = [remote(acc.at[pl.ds(0, hh), :, q_rows(far)], r1l, rs.at[0], rr.at[0], right),
          remote(acc.at[pl.ds(hh, hh), :, q_rows(far)], r1r, rs.at[1], rr.at[1], left)]
    for copy in p1:
        copy.start()

    def merge(a, b):
        ma, mb = a[:, HEAD_DIM:HEAD_DIM + 1, :], b[:, HEAD_DIM:HEAD_DIM + 1, :]
        m = jnp.maximum(ma, mb)
        wa, wb = jnp.exp2((ma - m) * EXP_SCALE), jnp.exp2((mb - m) * EXP_SCALE)
        o = a[:, 0:HEAD_DIM, :] * wa + b[:, 0:HEAD_DIM, :] * wb
        l = a[:, HEAD_DIM + 1:HEAD_DIM + 2, :] * wa + b[:, HEAD_DIM + 1:HEAD_DIM + 2, :] * wb
        return o, m, l

    def merge_into(lo, p, other):
        o, m, l = merge(acc[lo:lo + hh, :, q_rows(p)], other[...])
        acc[lo:lo + hh, 0:HEAD_DIM, q_rows(p)] = o
        acc[lo:lo + hh, HEAD_DIM:HEAD_DIM + 1, q_rows(p)] = m
        acc[lo:lo + hh, HEAD_DIM + 1:HEAD_DIM + 2, q_rows(p)] = l

    p1[0].wait_recv()
    merge_into(0, nxt, r1l)
    p1[1].wait_recv()
    merge_into(hh, prev, r1r)
    p2 = [remote(acc.at[:, :, q_rows(nxt)], r2l, rs.at[2], rr.at[2], right),
          remote(acc.at[:, :, q_rows(prev)], r2r, rs.at[3], rr.at[3], left)]
    for copy in p2:
        copy.start()
    for copy in p2:
        copy.wait_recv()
    for h in range(heads):
        a, b, d = acc[h:h + 1, :, q_rows(x)], r2l[h:h + 1], r2r[h:h + 1]
        o, m, l = merge(a, b)
        md = d[:, HEAD_DIM:HEAD_DIM + 1, :]
        top = jnp.maximum(m, md)
        w, wd = jnp.exp2((m - top) * EXP_SCALE), jnp.exp2((md - top) * EXP_SCALE)
        o = o * w + d[:, 0:HEAD_DIM, :] * wd
        l = l * w + d[:, HEAD_DIM + 1:HEAD_DIM + 2, :] * wd
        obuf[core, :, h * HEAD_DIM:(h + 1) * HEAD_DIM] = (o / l)[0].T.astype(BF16)
    swap = remote(obuf.at[core], obuf.at[core], os.at[0], orr.at[0], partner)
    swap.start()
    remote(obuf.at[1 - core], obuf.at[1 - core], os.at[0], orr.at[0], partner).wait_recv()
    o_out[:, 0:head_w] = obuf[0]
    o_out[:, head_w:2 * head_w] = obuf[1]
    for copy in x_copies + kv_copies + q_copies + p1 + p2 + [swap]:
        copy.wait_send()


def mlp_kernel(o_in, xres, gain, wo, wg, wu, wd, out,
               wov, wgv, wuv, wdv, part, r1l, r1r, r2l, r2r, hbuf, hres, ubuf, fin, fbuf,
               wosem, wgsem, wusem, wdsem, s1, q1, s2, q2, hs, hr, ps, pr, us, ur, fs, fr):
    me = Place()
    y, core = me.y, me.core
    nc, _, _, cw = part.shape
    half_w = nc * cw
    width = 2 * half_w
    rows = o_in.shape[0]
    block_rows = rows // RING
    nu, _, uw = wgv.shape
    half_f = nu * uw
    nd = wdv.shape[0]
    partner = me.at(other=True)
    up, down = me.at(dy=1), me.at(dy=-1 + RING)
    far, nxt, prev = (y + 2) % RING, (y + 1) % RING, (y + 3) % RING
    col0 = core * half_w

    def lanes(start, size):
        return pl.ds(pl.multiple_of(start, 128), size)

    def wo_copy(j):
        return pltpu.make_async_copy(wo.at[:, lanes(col0 + j * cw, cw)], wov.at[j], wosem.at[j])

    def wd_copy(j):
        return pltpu.make_async_copy(wd.at[:, lanes(col0 + j * cw, cw)], wdv.at[j % nd], wdsem.at[j % nd])

    def wg_copy(j):
        return pltpu.make_async_copy(wg.at[:, lanes(core * half_f + j * uw, uw)], wgv.at[j], wgsem.at[j])

    def wu_copy(j):
        return pltpu.make_async_copy(wu.at[:, lanes(core * half_f + j * uw, uw)], wuv.at[j], wusem.at[j])

    for j in range(nc):
        wo_copy(j).start()
    for j in range(nu):
        wg_copy(j).start()
        wu_copy(j).start()
    for j in range(nd):
        wd_copy(j).start()

    barrier([up, down, partner])

    hc = cw // 2

    def first_sends(j):
        return (remote(part.at[j, far, :, pl.ds(0, hc)], r1l.at[j], s1.at[0, j], q1.at[0, j], up),
                remote(part.at[j, far, :, pl.ds(hc, hc)], r1r.at[j], s1.at[1, j], q1.at[1, j], down))

    def second_sends(j):
        return (remote(part.at[j, nxt], r2l.at[j], s2.at[0, j], q2.at[0, j], up),
                remote(part.at[j, prev], r2r.at[j], s2.at[1, j], q2.at[1, j], down))

    def relay(j, carry):
        a, b = first_sends(j)
        a.wait_recv()
        part[j, nxt, :, 0:hc] = part[j, nxt, :, 0:hc] + r1l[j]
        b.wait_recv()
        part[j, prev, :, hc:cw] = part[j, prev, :, hc:cw] + r1r[j]
        for copy in second_sends(j):
            copy.start()
        return carry

    def total(j):
        for copy in second_sends(j):
            copy.wait_recv()
        return part[j, y] + r2l[j] + r2r[j]

    def drain(j, carry):
        for copy in first_sends(j) + second_sends(j):
            copy.wait_send()
        return carry

    attended = o_in[...]

    def out_chunk(j, carry):
        wo_copy(j).wait()
        part[j] = jnp.dot(attended, wov[j], preferred_element_type=F32).reshape(RING, block_rows, cw)
        for copy in first_sends(j):
            copy.start()
        return carry

    lax.fori_loop(0, nc, out_chunk, 0)
    lax.fori_loop(0, nc, relay, 0)

    def mid_chunk(j, carry):
        c = lanes(j * cw, cw)
        mid = (xres[:, c].astype(F32) + total(j)).astype(BF16)
        hres[:, c] = mid
        hbuf[core, y, :, c] = mid
        return carry

    lax.fori_loop(0, nc, mid_chunk, 0)
    h_copies = ring_gather(
        y, up, down, lambda p, c: hbuf.at[c, p], lambda p, c, i: hbuf.at[c, p, :, pl.ds(i * (half_w // 2), half_w // 2)],
        hs, hr, partner=partner, core=core, psends=ps, precvs=pr)
    for copy in h_copies:
        copy.wait_send()
    lax.fori_loop(0, nc, drain, 0)

    def norm_block(i, carry):
        v0, v1 = hbuf[0, i].astype(F32), hbuf[1, i].astype(F32)
        mean = (jnp.sum(v0 * v0, axis=-1, keepdims=True) + jnp.sum(v1 * v1, axis=-1, keepdims=True)) / width
        inv = lax.rsqrt(mean + NORM_EPS)
        hbuf[0, i] = (v0 * inv * gain[0:1, :].astype(F32)).astype(BF16)
        hbuf[1, i] = (v1 * inv * gain[1:2, :].astype(F32)).astype(BF16)
        return carry

    lax.fori_loop(0, RING, norm_block, 0)
    b0, b1 = hbuf[0].reshape(rows, half_w), hbuf[1].reshape(rows, half_w)

    def u_copy(j, c):
        at = ubuf.at[:, lanes(c * half_f + j * uw, uw)]
        return remote(at, at, us.at[j], ur.at[j], partner)

    def up_chunk(j, carry):
        wg_copy(j).wait()
        wu_copy(j).wait()
        gate = jnp.dot(b0, wgv[j, 0:half_w, :], preferred_element_type=F32) + jnp.dot(b1, wgv[j, half_w:width, :], preferred_element_type=F32)
        upper = jnp.dot(b0, wuv[j, 0:half_w, :], preferred_element_type=F32) + jnp.dot(b1, wuv[j, half_w:width, :], preferred_element_type=F32)
        ubuf[:, lanes(core * half_f + j * uw, uw)] = (jax.nn.silu(gate) * upper).astype(BF16)
        u_copy(j, core).start()
        return carry

    lax.fori_loop(0, nu, up_chunk, 0)
    for j in range(nu):
        u_copy(j, 1 - core).wait_recv()

    for j in range(nc):
        wd_copy(j).wait()
        part[j] = jnp.dot(ubuf[...], wdv[j % nd], preferred_element_type=F32).reshape(RING, block_rows, cw)
        if j + nd < nc:
            wd_copy(j + nd).start()
        for copy in first_sends(j):
            copy.start()
    lax.fori_loop(0, nc, relay, 0)

    def last_chunk(j, carry):
        c = lanes(j * cw, cw)
        fin[:, :, c] = (hres[:, c].astype(F32) + total(j)).astype(BF16).reshape(2, block_rows // 2, cw)
        return carry

    lax.fori_loop(0, nc, last_chunk, 0)
    swap = remote(fin.at[1 - core], fbuf.at[core], fs.at[0], fr.at[0], partner)
    swap.start()
    own = fin[core]
    out[:, lanes(col0, half_w)] = own
    remote(fin.at[core], fbuf.at[1 - core], fs.at[0], fr.at[0], partner).wait_recv()
    out[:, lanes((1 - core) * half_w, half_w)] = fbuf[1 - core]
    for j in range(nu):
        u_copy(j, core).wait_send()
    lax.fori_loop(0, nc, drain, 0)
    swap.wait_send()


def dma(*shape):
    return pltpu.SemaphoreType.DMA(shape)


def relative_positions(chips, shards, row_count):
    r = jnp.arange(row_count, dtype=jnp.int32)
    per_chip = 2 * RING * 16
    x = chips + r // per_chip
    y, core, w = (r % per_chip) // 32, (r % 32) // 16, r % 16
    k = (2 * x + core) * RING + y
    run = jnp.where(w < 8, k, 2 * shards - 1 - k)
    return run * 8 + w % 8


def solution(mesh):
    token_spec = P(('dp', 'cp', 'tp'), None)
    column_spec = P(None, 'tp')
    row_spec = P('tp', None)
    shards = mesh.shape['tp'] * mesh.shape['cp']

    def device_layer(hidden_loc, pos_loc, cache_len, cache_k, cache_v, norm1_gain, w_query, w_key, w_value, w_out, norm2_gain, w_gate, w_up, w_down):
        shard_rows, width = hidden_loc.shape
        half_w = width // 2
        chip_rows = 2 * RING * shard_rows
        rows = RING * chip_rows
        slots = cache_k.shape[0]
        head_w = w_query.shape[1] // 2
        heads = head_w // HEAD_DIM
        x = lax.axis_index('cp') // 2
        half = HEAD_DIM // 2
        relk = relative_positions(x, shards, chip_rows)
        relq = relative_positions(0, shards, rows)
        inv_freq = 1.0 / (ROPE_BASE ** (jnp.arange(half, dtype=F32) * (2.0 / HEAD_DIM)))
        angles = (cache_len[0] + relk).astype(F32)[:, None] * inv_freq[None, :]
        cos, sin = jnp.cos(angles), jnp.sin(angles)
        cos = jnp.concatenate([cos, cos], axis=1)
        sin = jnp.concatenate([-sin, sin], axis=1)
        block = (heads, HEAD_DIM + 8, chip_rows)
        part_block = (heads // 2,) + block[1:]
        attended, xres = pl.pallas_call(
            attention_kernel,
            out_shape=(jax.ShapeDtypeStruct((chip_rows, 2 * head_w), BF16), jax.ShapeDtypeStruct((2 * shard_rows, half_w), BF16)),
            in_specs=[ANY, SMEM, ANY, ANY, VMEM, ANY, ANY, ANY, VMEM, VMEM, VMEM, VMEM],
            out_specs=(VMEM, VMEM),
            scratch_shapes=[
                pltpu.VMEM((RING, 2, shard_rows, width), BF16),
                pltpu.VMEM((RING, 2 * shard_rows, width), BF16),
                pltpu.VMEM((width, head_w), BF16),
                pltpu.VMEM((width, HEAD_DIM), BF16),
                pltpu.VMEM((width, HEAD_DIM), BF16),
                pltpu.VMEM((2 * RING, slots, HEAD_DIM), BF16),
                pltpu.VMEM((2 * RING, slots, HEAD_DIM), BF16),
                pltpu.VMEM((HEAD_DIM, slots), BF16),
                pltpu.VMEM((rows, head_w), BF16),
                pltpu.VMEM((chip_rows, HEAD_DIM), BF16),
                pltpu.VMEM((chip_rows, HEAD_DIM), BF16),
                pltpu.VMEM((heads, HEAD_DIM + 8, rows), F32),
                pltpu.VMEM(part_block, F32),
                pltpu.VMEM(part_block, F32),
                pltpu.VMEM(block, F32),
                pltpu.VMEM(block, F32),
                pltpu.VMEM((2, chip_rows, head_w), BF16),
                dma(4), dma(4), dma(4), dma(4), dma(4), dma(2 * RING, 2), dma(2 * RING, 2),
                dma(4), dma(4), dma(4), dma(4), dma(1), dma(1),
            ],
            compiler_params=pltpu.CompilerParams(collective_id=0, has_side_effects=True, vmem_limit_bytes=48 * 2**20),
            name='attention',
        )(hidden_loc, cache_len, cache_k, cache_v, norm1_gain.reshape(1, width), w_query, w_key, w_value, cos, sin, relq.reshape(1, rows), relk.reshape(chip_rows, 1))

        cw = 512 if half_w % 512 == 0 and half_w > 512 else 256
        nc = half_w // cw
        half_f = w_gate.shape[1] // 2
        uw = 256
        nu = half_f // uw
        nd = max(1, nc - 1)
        br = 2 * shard_rows
        return pl.pallas_call(
            mlp_kernel,
            out_shape=jax.ShapeDtypeStruct((shard_rows, width), BF16),
            in_specs=[VMEM, VMEM, VMEM, ANY, ANY, ANY, ANY],
            out_specs=VMEM,
            scratch_shapes=[
                pltpu.VMEM((nc, 2 * head_w, cw), BF16),
                pltpu.VMEM((nu, width, uw), BF16),
                pltpu.VMEM((nu, width, uw), BF16),
                pltpu.VMEM((nd, 2 * half_f, cw), BF16),
                pltpu.VMEM((nc, RING, br, cw), F32),
                pltpu.VMEM((nc, br, cw // 2), F32),
                pltpu.VMEM((nc, br, cw // 2), F32),
                pltpu.VMEM((nc, br, cw), F32),
                pltpu.VMEM((nc, br, cw), F32),
                pltpu.VMEM((2, RING, br, half_w), BF16),
                pltpu.VMEM((br, half_w), BF16),
                pltpu.VMEM((chip_rows, 2 * half_f), BF16),
                pltpu.VMEM((2, shard_rows, half_w), BF16),
                pltpu.VMEM((2, shard_rows, half_w), BF16),
                dma(nc), dma(nu), dma(nu), dma(nd), dma(2, nc), dma(2, nc), dma(2, nc), dma(2, nc),
                dma(4), dma(4), dma(4), dma(4), dma(nu), dma(nu), dma(1), dma(1),
            ],
            compiler_params=pltpu.CompilerParams(collective_id=1, has_side_effects=True, vmem_limit_bytes=67043328),
            name='mlp',
        )(attended, xres, norm2_gain.reshape(2, half_w), w_out, w_gate, w_up, w_down)

    return jax.shard_map(device_layer, mesh=mesh, in_specs=(token_spec, P(('dp', 'cp', 'tp')), P('dp'), token_spec, token_spec, P(), column_spec, column_spec, column_spec, row_spec, P(), column_spec, column_spec, row_spec), out_specs=token_spec, check_vma=False)
```

time: 520 us -> 175 us (0.34)
  Pallas kernels: 0 us -> 164 us
  matrix products: 160 us -> 0 us
  blocking collectives: 145 us -> 0 us
  local copies, waits for them, and re-layouts: 106 us -> 8.36 us
  waiting for transfers between devices: 48.1 us -> 0 us
  other arithmetic: 40.4 us -> 0.51 us
  between operations: 14.7 us -> 0.74 us
    pallas_call x0 -> x2, Pallas kernels: none -> 164 us  [the longest x1 98.3 us: device_layer(): pl.pallas_call(attention_kernel, out_shape=(jax.ShapeDtypeStruct((chip_ro...]
    dot_general x22 -> x0, matrix products: 160 us -> none  [the longest x4 50.8 us: attend_rows(): jnp.einsum('rkgd,skd->krgs', block_queries, cache_keys, preferred_element...]
    all_gather x4 -> x0, blocking collectives: 66.1 us -> none  [the longest x1 25.2 us: device_layer(): new_values = lax.all_gather(values_loc, 'cp', axis=0, tiled=True)]
    all_to_all x2 -> x0, blocking collectives: 60.4 us -> none  [the longest x1 31.3 us: device_layer(): lax.all_to_all(cache_k, 'tp', 1, 0, tiled=True)]
    unnamed x32 -> x13, local copies, waits for them, and re-layouts: 52.2 us -> 7.04 us
    reduce_scatter x2 -> x0, waiting for transfers between devices: 45 us -> none  [the longest x1 24 us: device_layer(): lax.psum_scatter(mlp_part, 'tp', scatter_dimension=0, tiled=True)]
    all_gather x2 -> x0, local copies, waits for them, and re-layouts: 42.5 us -> none  [the longest x1 21.3 us: device_layer(): lax.all_gather(lax.all_to_all(cache_k, 'tp', 1, 0, tiled=True), 'cp', axi...]
    reduce_sum x10 -> x0, other arithmetic: 34.9 us -> none  [the longest x4 32.9 us: attend_rows(): jnp.sum(cache_probs, axis=-1, keepdims=True)]
  transfers between devices with their start and end apart: 4 -> 0, of which waited for: 3 -> 0; matrix products, arithmetic and copies ran while one was open for 12% -> 0% of each run, Pallas kernels for 0% -> 0%
where the time goes in v1:
time: 175 us; the launch traced here: 174 us
  Pallas kernels  164 us (94%)
  local copies, waits for them, and re-layouts  8.36 us (5%)
    pallas_call x1, Pallas kernels, device_layer(): pl.pallas_call(attention_kernel, out_shape=(jax.ShapeDtypeStruct((chip_ro...  98.3 us
    pallas_call x1, Pallas kernels, device_layer(): pl.pallas_call(mlp_kernel, out_shape=jax.ShapeDtypeStruct((shard_rows, wi...  66.1 us
    unnamed x13, local copies, waits for them, and re-layouts  7.04 us

profile of v1, /device:TPU:99, one launch (start us, length us, event | category | flops | bytes accessed | tf_op | source)
XLA Modules:
  0.0 174.0 jit_solution(13618417306782942820)
XLA Ops:
  0.0 0.0 copy-start.5
  0.7 0.3 fusion.29
  1.0 0.1 pad_maximum_fusion
  1.2 0.7 reshape.503.gain
  1.9 0.0 copy-start
  1.9 1.6 copy-done
  3.5 0.0 copy-start.1
  3.5 1.6 copy-done.1
  5.1 0.0 copy-start.3
  5.1 0.9 copy-done.3
  6.0 98.3 %attention.1 = (bf16[128,1024]{1,0:T(8,128)(2,1)S(1)}, bf16[32,2560]{1,0:T(8,128)(2,1)S(1)}) custom-call(bf16[16,5120]{1,0:T(8,128)(2,1)S(1)} %copy-done.3, s32[1]{0:T(128)} %copy.15.len_ref, bf16[1024,1024]{1,0:T(8,128)(2,1)S(1)} %copy-done, bf16[1024,1024]{1,0:T(8,128)(2,1)S(1)} %copy-done.1, bf16[1,5120]{1,0:T(2,128)(2,1)S(1)} %reshape.503.gain, ...), custom_call_target="tpu_custom_call" | custom-call | tf_op jit(solution)/shard_map/attention/pallas_call | solution.py:462
  104.4 0.0 copy-start.2
  104.4 0.7 copy-done.2
  105.1 0.0 copy-start.4
  105.1 0.7 copy-done.4
  105.8 0.0 copy-done.5
  105.8 0.6 reshape.504.gain
  106.4 66.1 %mlp.1 = bf16[16,5120]{1,0:T(8,128)(2,1)} custom-call(bf16[128,1024]{1,0:T(8,128)(2,1)} %copy-done.2, bf16[32,2560]{1,0:T(8,128)(2,1)} %copy-done.4, bf16[2,2560]{1,0:T(2,128)(2,1)} %reshape.504.gain, bf16[1024,5120]{1,0:T(8,128)(2,1)} %wo.1, bf16[5120,3584]{1,0:T(8,128)(2,1)} %wg.1, bf16[5120,3584]{1,0:T(8,128)(2,1)} %wu.1, bf16[3584,5120]{1,0:T(8,128)(2,1)} %wd.1), custom_call_target="tpu_custom_call" | custom-call | tf_op jit(solution)/shard_map/mlp/pallas_call | solution.py:499
  172.5 1.6 copy.16
  (4 shorter events, 0.1 us)
Async XLA Ops:
  0.0 105.8 %copy-start.5 = (bf16[5120]{0:T(1024)(128)(2,1)S(1)}, bf16[5120]{0:T(1024)(128)(2,1)}, u32[]{:S(2)}) copy-start(bf16[5120]{0:T(1024)(128)(2,1)} %param.23) | copy-start | bytes 30724
  1.9 1.6 copy-start
  3.5 1.6 copy-start.1
  5.1 0.9 copy-start.3
  104.4 0.7 copy-start.2
  105.1 0.7 copy-start.4

commit v2 on v1

--- a/solution.py
+++ b/solution.py
@@ -13,9 +13,11 @@
 MESH = pl.DeviceIdType.MESH
 F32 = jnp.float32
 BF16 = jnp.bfloat16
-M_INIT = -3e38
+M_INIT = -1e38
+MASKED = -3e38
 EXP_SCALE = math.log2(math.e) / math.sqrt(HEAD_DIM)
 RING = 4
+STEP = 512
 ANY = pl.BlockSpec(memory_space=pl.ANY)
 VMEM = pl.BlockSpec(memory_space=pltpu.VMEM)
 SMEM = pl.BlockSpec(memory_space=pltpu.SMEM)
@@ -27,10 +29,14 @@
         cp = lax.axis_index('cp')
         self.x = cp // 2
         self.core = cp % 2
-
-    def at(self, dx=0, dy=0, other=False):
-        core = 1 - self.core if other else self.core
-        return {'tp': (self.y + dy) % RING, 'cp': ((self.x + dx) % RING) * 2 + core}
+        self.vx = self.x + self.core * (self.y - self.x)
+        self.vy = self.y + self.core * (self.x - self.y)
+
+    def at(self, dx=0, dy=0, core=None):
+        return {'tp': (self.y + dy) % RING, 'cp': ((self.x + dx) % RING) * 2 + (self.core if core is None else core)}
+
+    def mirrored(self, core):
+        return {'tp': self.x, 'cp': self.y * 2 + core}
 
 
 def remote(src, dst, send_sem, recv_sem, device):
@@ -82,10 +88,10 @@
 
 
 def attention_kernel(x_in, len_ref, ck, cv, gain, wq, wk, wv, cos_ref, sin_ref, relq_ref, relk_ref, o_out, xres_out,
-                     xbuf, abuf, wqv, wkv, wvv, kbuf, vbuf, vt, qall, knew, vnew, acc, r1l, r1r, r2l, r2r, obuf,
-                     lsem, xs, xr, ps, pr, kvs, kvr, qs, qr, rs, rr, os, orr):
+                     xbuf, abuf, wqv, wkv, wvv, kbuf, vbuf, rk, rv, kaug, vt, qkv, qall, qaug, sa, sb, acc, r1l, r1r, r2l, r2r, otmp, obuf,
+                     lsem, xs, xr, ps, pr, kvs, kvr, relay_r, ts, tr, qs, qr, rs, rr, os, orr):
     me = Place()
-    x, y, core = me.x, me.y, me.core
+    x, y, core, vx, vy = me.x, me.y, me.core, me.vx, me.vy
     width = x_in.shape[1]
     half_w = width // 2
     slots = ck.shape[0]
@@ -93,10 +99,11 @@
     chip_rows = rows // RING
     heads = acc.shape[0]
     head_w = heads * HEAD_DIM
-    col = [(dy, dk) for dy in (0, 1, 3, 2) for dk in (0, 1)]
-    partner = me.at(other=True)
-    up, down = me.at(dy=1), me.at(dy=-1 + RING)
-    right, left = me.at(dx=1), me.at(dx=-1 + RING)
+    partner = me.at(core=1 - core)
+    up, down = me.at(dy=1), me.at(dy=RING - 1)
+    right, left = me.at(dx=1 - core, dy=core), me.at(dx=(1 - core) * (RING - 1), dy=core * (RING - 1))
+    ahead, behind = me.at(dx=core, dy=1 - core), me.at(dx=core * (RING - 1), dy=(1 - core) * (RING - 1))
+    moving = jnp.logical_and(core == 1, x != y)
 
     local = [
         pltpu.make_async_copy(x_in, xbuf.at[y, core], lsem.at[0]),
@@ -107,25 +114,49 @@
     for copy in local:
         copy.start()
 
-    barrier([me.at(dy=dy, other=bool(dk)) for dy, dk in col[1:]] + [right, left])
+    peers = [partner, me.mirrored(0), me.mirrored(1)]
+    peers += [me.at(dy=d, core=c) for d in range(1, RING) for c in range(2)] + [me.at(dx=d, core=c) for d in range(1, RING) for c in range(2)]
+    barrier(peers)
+
+    def kv_lanes(head):
+        return pl.ds(pl.multiple_of(head * HEAD_DIM, HEAD_DIM), HEAD_DIM)
+
+    def target(role, d):
+        return me.at(dx=d if role else 0, dy=0 if role else d, core=role)
+
+    def target_lanes(role, d):
+        return kv_lanes(2 * (((x if role else y) + d) % RING) + role)
 
     kv_copies = []
 
-    def send_kv():
-        for s, (dy, dk) in enumerate(col):
-            head = 2 * ((y + dy) % RING) + (1 - core if dk else core)
-            lanes = pl.ds(pl.multiple_of(head * HEAD_DIM, HEAD_DIM), HEAD_DIM)
-            for i, (src, dst) in enumerate(((ck, kbuf), (cv, vbuf))):
-                if s == 0:
-                    copy = pltpu.make_async_copy(src.at[:, lanes], dst.at[s], kvr.at[s, i])
-                else:
-                    copy = remote(src.at[:, lanes], dst.at[s], kvs.at[s, i], kvr.at[s, i], me.at(dy=dy, other=bool(dk)))
-                    kv_copies.append(copy)
-                copy.start()
+    def kv_send(src, dst, recv, device):
+        copy = remote(src, dst, kvs.at[len(kv_copies)], recv, device)
+        copy.start()
+        kv_copies.append(copy)
+
+    def send_near():
+        other_vy = x + y - vy
+        for i, (src, dst) in enumerate(((ck, kbuf), (cv, vbuf))):
+            pltpu.make_async_copy(src.at[:, kv_lanes(2 * vy + core)], dst.at[core], kvr.at[core, i]).start()
+            kv_send(src.at[:, kv_lanes(2 * other_vy + 1 - core)], dst.at[core], kvr.at[core, i], partner)
+        for role in range(2):
+            kv_send(ck.at[:, target_lanes(role, 2)], rk.at[core], relay_r.at[0, core], target(role, 1))
+            kv_send(cv.at[:, target_lanes(role, 2)], rv.at[core], relay_r.at[1, core], target(role, RING - 1))
+
+    def send_far():
+        for i, (src, dst) in enumerate(((ck, kbuf), (cv, vbuf))):
+            for role in range(2):
+                for d, slot in ((1, 2), (3, 4)):
+                    kv_send(src.at[:, target_lanes(role, d)], dst.at[slot + core], kvr.at[slot + core, i], target(role, d))
+        for c in range(2):
+            remote(rk.at[c], rk.at[c], kvs.at[0], relay_r.at[0, c], behind).wait_recv()
+            kv_send(rk.at[c], kbuf.at[6 + c], kvr.at[6 + c, 0], ahead)
+            remote(rv.at[c], rv.at[c], kvs.at[0], relay_r.at[1, c], ahead).wait_recv()
+            kv_send(rv.at[c], vbuf.at[6 + c], kvr.at[6 + c, 1], behind)
 
     x_copies = ring_gather(
         y, up, down, lambda p, c: xbuf.at[p, c], lambda p, c, i: xbuf.at[p, c, :, pl.ds(i * half_w, half_w)],
-        xs, xr, own=x_in, partner=partner, core=core, psends=ps, precvs=pr, between=send_kv)
+        xs, xr, own=x_in, partner=partner, core=core, psends=ps, precvs=pr, between=send_near)
     local[0].wait()
 
     def norm_block(i, carry):
@@ -145,38 +176,58 @@
     def rotate(v):
         return (v * cos + pltpu.roll(v, HEAD_DIM // 2, 1) * sin).astype(BF16)
 
-    my_rows = pl.ds(pl.multiple_of(x * chip_rows, chip_rows), chip_rows)
     q = jnp.dot(normed, wqv[...], preferred_element_type=F32)
     for h in range(heads):
-        qall[my_rows, h * HEAD_DIM:(h + 1) * HEAD_DIM] = rotate(q[:, h * HEAD_DIM:(h + 1) * HEAD_DIM])
-    knew[...] = rotate(jnp.dot(normed, wkv[...], preferred_element_type=F32))
-    vnew[...] = jnp.dot(normed, wvv[...], preferred_element_type=F32).astype(BF16)
+        qkv[:, h * HEAD_DIM:(h + 1) * HEAD_DIM] = rotate(q[:, h * HEAD_DIM:(h + 1) * HEAD_DIM])
+    qkv[:, head_w:head_w + HEAD_DIM] = rotate(jnp.dot(normed, wkv[...], preferred_element_type=F32))
+    qkv[:, head_w + HEAD_DIM:] = jnp.dot(normed, wvv[...], preferred_element_type=F32).astype(BF16)
 
     def q_rows(p):
         return pl.ds(pl.multiple_of(p * chip_rows, chip_rows), chip_rows)
 
+    across_in = remote(qkv, qall.at[q_rows(vx)], ts.at[0], tr.at[0], me.mirrored(core))
+    mirror_send = remote(qkv, qall.at[q_rows(x)], ts.at[0], tr.at[0], me.mirrored(core))
+
+    @pl.when(moving)
+    def _():
+        mirror_send.start()
+        across_in.wait_recv()
+
+    @pl.when(jnp.logical_not(moving))
+    def _():
+        qall[q_rows(vx), :] = qkv[...]
+
     q_copies = ring_gather(
-        x, right, left, lambda p, c: qall.at[q_rows(p), :],
-        lambda p, c, i: qall.at[q_rows(p), pl.ds(i * head_w // 2, head_w // 2)], qs, qr)
+        vx, right, left, lambda p, c: qall.at[q_rows(p), pl.ds(0, head_w)],
+        lambda p, c, i: qall.at[q_rows(p), pl.ds(i * (head_w // 2), head_w // 2)], qs, qr, between=send_far)
+
+    first_lane = jnp.where(lax.broadcasted_iota(jnp.int32, (rows, HEAD_DIM), 1) == 0, 1.0, 0.0).astype(BF16)
+    for h in range(heads):
+        qaug[h, :, 0:HEAD_DIM] = qall[:, h * HEAD_DIM:(h + 1) * HEAD_DIM]
+        qaug[h, :, HEAD_DIM:] = first_lane
 
     tile = 256
     tiles = rows // tile
-
-    def softmax_step(keys, vt_value, h, j, mask_of, first):
+    contract_last = (((1,), (1,)), ((), ()))
+
+    def finish(s_ref, e_top, vt_ref, h, j, first, depth):
         lanes = pl.ds(j * tile, tile)
-        queries = qall[j * tile:(j + 1) * tile, pl.ds(pl.multiple_of(h * HEAD_DIM, HEAD_DIM), HEAD_DIM)]
-        s = lax.dot_general(keys, queries, (((1,), (1,)), ((), ())), preferred_element_type=F32)
-        s = jnp.where(mask_of(j, s.shape), s, -jnp.inf)
-        top = jnp.max(s, axis=0, keepdims=True)
         if first:
-            m_new = jnp.maximum(top, M_INIT)
+            m_new = jnp.maximum(e_top, M_INIT)
         else:
             m_old = acc[h, HEAD_DIM:HEAD_DIM + 1, lanes]
             l_old = acc[h, HEAD_DIM + 1:HEAD_DIM + 2, lanes]
-            m_new = jnp.maximum(top, m_old)
-        e = jnp.exp2(s * EXP_SCALE - m_new * EXP_SCALE)
-        l_new = jnp.sum(e, axis=0, keepdims=True)
-        o = jnp.dot(vt_value, e.astype(BF16), preferred_element_type=F32)
+            m_new = jnp.maximum(e_top, m_old)
+        m_scaled = m_new * EXP_SCALE
+        part_l, o = None, None
+        step = min(STEP, depth)
+        for k in range(0, depth, step):
+            e = jnp.exp2(s_ref[k:k + step, :] * EXP_SCALE - m_scaled)
+            total_e = jnp.sum(e.reshape(step // 8, 8, tile), axis=0)
+            part_l = total_e if part_l is None else part_l + total_e
+            term = jnp.dot(vt_ref[:, k:k + step], e.astype(BF16), preferred_element_type=F32)
+            o = term if o is None else o + term
+        l_new = jnp.sum(part_l, axis=0, keepdims=True)
         if not first:
             alpha = jnp.exp2((m_old - m_new) * EXP_SCALE)
             l_new = l_new + l_old * alpha
@@ -185,39 +236,55 @@
         acc[h, HEAD_DIM:HEAD_DIM + 1, lanes] = m_new
         acc[h, HEAD_DIM + 1:HEAD_DIM + 2, lanes] = l_new
 
-    vnew_t = vnew[...].astype(F32).T.astype(BF16)
+    my_rows = q_rows(vx)
+    vnew_t = qall[my_rows, head_w + HEAD_DIM:].T
+    knew = qall[my_rows, head_w:head_w + HEAD_DIM]
     relk = relk_ref[...]
 
     def new_head(h, carry):
         for j in range(tiles):
-            softmax_step(knew[...], vnew_t, h, j, lambda j, shape: jnp.broadcast_to(relk, shape) <= jnp.broadcast_to(relq_ref[:, j * tile:(j + 1) * tile], shape), True)
+            s = lax.dot_general(knew, qaug[h, j * tile:(j + 1) * tile, 0:HEAD_DIM], contract_last, preferred_element_type=F32)
+            causal = jnp.broadcast_to(relk, s.shape) <= jnp.broadcast_to(relq_ref[:, j * tile:(j + 1) * tile], s.shape)
+            s = jnp.where(causal, s, -jnp.inf)
+            finish(s, jnp.max(s, axis=0, keepdims=True), vnew_t, h, j, True, chip_rows)
         return carry
 
     lax.fori_loop(0, heads, new_head, 0)
     cache_len = len_ref[0]
+    slot_ids = lax.broadcasted_iota(jnp.int32, (slots, HEAD_DIM), 0)
+
+    def scores(h, j, dst):
+        s = lax.dot_general(kaug[...], qaug[h, j * tile:(j + 1) * tile, :], contract_last, preferred_element_type=F32)
+        dst[...] = s
+        return jnp.max(s, axis=0, keepdims=True)
 
     def source(s, carry):
-        u, dk = s // 2, s % 2
-        dy = u + (u // 2) * (1 - 2 * (u % 2))
-        src_core = core + dk * (1 - 2 * core)
-        src_y = (y - dy + RING) % RING
-        base = ((2 * x + src_core) * RING + src_y) * slots
+        u, src_core = s // 2, s % 2
+        d = u + (u // 2) * (1 - 2 * (u % 2))
+        src_x = (x - core * d + RING) % RING
+        src_y = (y - (1 - core) * d + RING) % RING
+        base = ((2 * src_x + src_core) * RING + src_y) * slots
         for i, (src, dst) in enumerate(((ck, kbuf), (cv, vbuf))):
             pltpu.make_async_copy(src.at[:, pl.ds(0, HEAD_DIM)], dst.at[s], kvr.at[s, i]).wait()
-        vt[...] = vbuf[s].astype(F32).T.astype(BF16)
-        seen = cache_len - base
-
-        def head(h, c):
-            for j in range(tiles):
-                softmax_step(kbuf[s], vt[...], h, j, lambda j, shape: lax.broadcasted_iota(jnp.int32, shape, 0) < seen, False)
-            return c
-
-        return lax.fori_loop(0, heads, head, carry)
-
-    lax.fori_loop(0, len(col), source, 0)
+        vt[...] = vbuf[s].T
+        seen = slot_ids < cache_len - base
+        kaug[:, 0:HEAD_DIM] = jnp.where(seen, kbuf[s].astype(F32), 0.0).astype(BF16)
+        kaug[:, HEAD_DIM:] = jnp.where(seen, 0.0, MASKED).astype(BF16)
+
+        def head(h, top_a):
+            top_b = scores(h, 1, sb)
+            finish(sa, top_a, vt, h, 0, False, slots)
+            top_a = scores(jnp.minimum(h + 1, heads - 1), 0, sa)
+            finish(sb, top_b, vt, h, 1, False, slots)
+            return top_a
+
+        lax.fori_loop(0, heads, head, scores(0, 0, sa))
+        return carry
+
+    lax.fori_loop(0, 2 * RING, source, 0)
 
     hh = heads // 2
-    far, nxt, prev = (x + 2) % RING, (x + 1) % RING, (x + 3) % RING
+    far, nxt, prev = (vx + 2) % RING, (vx + 1) % RING, (vx + 3) % RING
     p1 = [remote(acc.at[pl.ds(0, hh), :, q_rows(far)], r1l, rs.at[0], rr.at[0], right),
           remote(acc.at[pl.ds(hh, hh), :, q_rows(far)], r1r, rs.at[1], rr.at[1], left)]
     for copy in p1:
@@ -237,32 +304,50 @@
         acc[lo:lo + hh, HEAD_DIM:HEAD_DIM + 1, q_rows(p)] = m
         acc[lo:lo + hh, HEAD_DIM + 1:HEAD_DIM + 2, q_rows(p)] = l
 
+    p2 = [remote(acc.at[:, :, q_rows(nxt)], r2l, rs.at[2], rr.at[2], right),
+          remote(acc.at[:, :, q_rows(prev)], r2r, rs.at[3], rr.at[3], left)]
     p1[0].wait_recv()
     merge_into(0, nxt, r1l)
+    p2[0].start()
     p1[1].wait_recv()
     merge_into(hh, prev, r1r)
-    p2 = [remote(acc.at[:, :, q_rows(nxt)], r2l, rs.at[2], rr.at[2], right),
-          remote(acc.at[:, :, q_rows(prev)], r2r, rs.at[3], rr.at[3], left)]
-    for copy in p2:
-        copy.start()
+    p2[1].start()
     for copy in p2:
         copy.wait_recv()
     for h in range(heads):
-        a, b, d = acc[h:h + 1, :, q_rows(x)], r2l[h:h + 1], r2r[h:h + 1]
+        a, b, d = acc[h:h + 1, :, q_rows(vx)], r2l[h:h + 1], r2r[h:h + 1]
         o, m, l = merge(a, b)
         md = d[:, HEAD_DIM:HEAD_DIM + 1, :]
         top = jnp.maximum(m, md)
         w, wd = jnp.exp2((m - top) * EXP_SCALE), jnp.exp2((md - top) * EXP_SCALE)
         o = o * w + d[:, 0:HEAD_DIM, :] * wd
         l = l * w + d[:, HEAD_DIM + 1:HEAD_DIM + 2, :] * wd
-        obuf[core, :, h * HEAD_DIM:(h + 1) * HEAD_DIM] = (o / l)[0].T.astype(BF16)
-    swap = remote(obuf.at[core], obuf.at[core], os.at[0], orr.at[0], partner)
-    swap.start()
-    remote(obuf.at[1 - core], obuf.at[1 - core], os.at[0], orr.at[0], partner).wait_recv()
+        otmp[:, h * HEAD_DIM:(h + 1) * HEAD_DIM] = (o / l)[0].T.astype(BF16)
+
+    other_at = {'tp': vy, 'cp': vx * 2 + 1 - core}
+    other_out = remote(otmp, obuf.at[core], os.at[1], orr.at[1], other_at)
+    other_out.start()
+    same_out = remote(otmp, obuf.at[core], os.at[0], orr.at[0], me.mirrored(core))
+
+    @pl.when(moving)
+    def _():
+        same_out.start()
+        same_out.wait_recv()
+
+    @pl.when(jnp.logical_not(moving))
+    def _():
+        obuf[core] = otmp[...]
+
+    remote(otmp, obuf.at[1 - core], os.at[1], orr.at[1], partner).wait_recv()
     o_out[:, 0:head_w] = obuf[0]
     o_out[:, head_w:2 * head_w] = obuf[1]
-    for copy in x_copies + kv_copies + q_copies + p1 + p2 + [swap]:
+    for copy in x_copies + kv_copies + q_copies + p1 + p2 + [other_out]:
         copy.wait_send()
+
+    @pl.when(moving)
+    def _():
+        mirror_send.wait_send()
+        same_out.wait_send()
 
 
 def mlp_kernel(o_in, xres, gain, wo, wg, wu, wd, out,
@@ -278,8 +363,8 @@
     nu, _, uw = wgv.shape
     half_f = nu * uw
     nd = wdv.shape[0]
-    partner = me.at(other=True)
-    up, down = me.at(dy=1), me.at(dy=-1 + RING)
+    partner = me.at(core=1 - core)
+    up, down = me.at(dy=1), me.at(dy=RING - 1)
     far, nxt, prev = (y + 2) % RING, (y + 1) % RING, (y + 3) % RING
     col0 = core * half_w
 
@@ -350,19 +435,62 @@
     lax.fori_loop(0, nc, out_chunk, 0)
     lax.fori_loop(0, nc, relay, 0)
 
+    def h_piece(c, p, j):
+        return hbuf.at[c, p, :, lanes(j * cw, cw)]
+
+    def h_half(c, p, j, i):
+        return hbuf.at[c, p, :, lanes(j * cw + i * hc, hc)]
+
+    def h_steps(j):
+        return (remote(h_piece(core, y, j), h_piece(core, y, j), hs.at[0, j], hr.at[0, j], up),
+                remote(h_piece(core, y, j), h_piece(core, y, j), hs.at[1, j], hr.at[1, j], down),
+                remote(h_half(core, prev, j, 0), h_half(core, prev, j, 0), hs.at[2, j], hr.at[2, j], up),
+                remote(h_half(core, nxt, j, 1), h_half(core, nxt, j, 1), hs.at[3, j], hr.at[3, j], down))
+
+    def h_give(j, i, p, c):
+        return remote(h_piece(c, p, j), h_piece(c, p, j), ps.at[i, j], pr.at[i, j], partner)
+
     def mid_chunk(j, carry):
         c = lanes(j * cw, cw)
         mid = (xres[:, c].astype(F32) + total(j)).astype(BF16)
         hres[:, c] = mid
         hbuf[core, y, :, c] = mid
+        for copy in h_steps(j)[:2] + (h_give(j, 0, y, core),):
+            copy.start()
         return carry
 
     lax.fori_loop(0, nc, mid_chunk, 0)
-    h_copies = ring_gather(
-        y, up, down, lambda p, c: hbuf.at[c, p], lambda p, c, i: hbuf.at[c, p, :, pl.ds(i * (half_w // 2), half_w // 2)],
-        hs, hr, partner=partner, core=core, psends=ps, precvs=pr)
-    for copy in h_copies:
-        copy.wait_send()
+
+    def h_forward(j, carry):
+        steps = h_steps(j)
+        remote(h_piece(core, prev, j), h_piece(core, prev, j), hs.at[0, j], hr.at[0, j], down).wait_recv()
+        steps[2].start()
+        h_give(j, 1, prev, core).start()
+        remote(h_piece(core, nxt, j), h_piece(core, nxt, j), hs.at[1, j], hr.at[1, j], up).wait_recv()
+        steps[3].start()
+        h_give(j, 2, nxt, core).start()
+        return carry
+
+    lax.fori_loop(0, nc, h_forward, 0)
+
+    def h_last(j, carry):
+        remote(h_half(core, far, j, 0), h_half(core, far, j, 0), hs.at[2, j], hr.at[2, j], down).wait_recv()
+        remote(h_half(core, far, j, 1), h_half(core, far, j, 1), hs.at[3, j], hr.at[3, j], up).wait_recv()
+        h_give(j, 3, far, core).start()
+        return carry
+
+    lax.fori_loop(0, nc, h_last, 0)
+
+    def h_end(j, carry):
+        for i, p in enumerate((y, prev, nxt, far)):
+            h_give(j, i, p, 1 - core).wait_recv()
+        for copy in h_steps(j):
+            copy.wait_send()
+        for i, p in enumerate((y, prev, nxt, far)):
+            h_give(j, i, p, core).wait_send()
+        return carry
+
+    lax.fori_loop(0, nc, h_end, 0)
     lax.fori_loop(0, nc, drain, 0)
 
     def norm_block(i, carry):
@@ -448,12 +576,13 @@
         slots = cache_k.shape[0]
         head_w = w_query.shape[1] // 2
         heads = head_w // HEAD_DIM
-        x = lax.axis_index('cp') // 2
+        cp, y = lax.axis_index('cp'), lax.axis_index('tp')
         half = HEAD_DIM // 2
-        relk = relative_positions(x, shards, chip_rows)
+        own_rel = relative_positions(cp // 2, shards, chip_rows)
+        relk = relative_positions(jnp.where(cp % 2 == 0, cp // 2, y), shards, chip_rows)
         relq = relative_positions(0, shards, rows)
         inv_freq = 1.0 / (ROPE_BASE ** (jnp.arange(half, dtype=F32) * (2.0 / HEAD_DIM)))
-        angles = (cache_len[0] + relk).astype(F32)[:, None] * inv_freq[None, :]
+        angles = (cache_len[0] + own_rel).astype(F32)[:, None] * inv_freq[None, :]
         cos, sin = jnp.cos(angles), jnp.sin(angles)
         cos = jnp.concatenate([cos, cos], axis=1)
         sin = jnp.concatenate([-sin, sin], axis=1)
@@ -472,20 +601,26 @@
                 pltpu.VMEM((width, HEAD_DIM), BF16),
                 pltpu.VMEM((2 * RING, slots, HEAD_DIM), BF16),
                 pltpu.VMEM((2 * RING, slots, HEAD_DIM), BF16),
+                pltpu.VMEM((2, slots, HEAD_DIM), BF16),
+                pltpu.VMEM((2, slots, HEAD_DIM), BF16),
+                pltpu.VMEM((slots, 2 * HEAD_DIM), BF16),
                 pltpu.VMEM((HEAD_DIM, slots), BF16),
-                pltpu.VMEM((rows, head_w), BF16),
-                pltpu.VMEM((chip_rows, HEAD_DIM), BF16),
-                pltpu.VMEM((chip_rows, HEAD_DIM), BF16),
+                pltpu.VMEM((chip_rows, head_w + 2 * HEAD_DIM), BF16),
+                pltpu.VMEM((rows, head_w + 2 * HEAD_DIM), BF16),
+                pltpu.VMEM((heads, rows, 2 * HEAD_DIM), BF16),
+                pltpu.VMEM((slots, 256), F32),
+                pltpu.VMEM((slots, 256), F32),
                 pltpu.VMEM((heads, HEAD_DIM + 8, rows), F32),
                 pltpu.VMEM(part_block, F32),
                 pltpu.VMEM(part_block, F32),
                 pltpu.VMEM(block, F32),
                 pltpu.VMEM(block, F32),
+                pltpu.VMEM((chip_rows, head_w), BF16),
                 pltpu.VMEM((2, chip_rows, head_w), BF16),
-                dma(4), dma(4), dma(4), dma(4), dma(4), dma(2 * RING, 2), dma(2 * RING, 2),
-                dma(4), dma(4), dma(4), dma(4), dma(1), dma(1),
+                dma(4), dma(4), dma(4), dma(4), dma(4), dma(18), dma(2 * RING, 2), dma(2, 2), dma(1), dma(1),
+                dma(4), dma(4), dma(4), dma(4), dma(2), dma(2),
             ],
-            compiler_params=pltpu.CompilerParams(collective_id=0, has_side_effects=True, vmem_limit_bytes=48 * 2**20),
+            compiler_params=pltpu.CompilerParams(collective_id=0, has_side_effects=True, vmem_limit_bytes=67043328),
             name='attention',
         )(hidden_loc, cache_len, cache_k, cache_v, norm1_gain.reshape(1, width), w_query, w_key, w_value, cos, sin, relq.reshape(1, rows), relk.reshape(chip_rows, 1))
 
@@ -517,7 +652,7 @@
                 pltpu.VMEM((2, shard_rows, half_w), BF16),
                 pltpu.VMEM((2, shard_rows, half_w), BF16),
                 dma(nc), dma(nu), dma(nu), dma(nd), dma(2, nc), dma(2, nc), dma(2, nc), dma(2, nc),
-                dma(4), dma(4), dma(4), dma(4), dma(nu), dma(nu), dma(1), dma(1),
+                dma(4, nc), dma(4, nc), dma(4, nc), dma(4, nc), dma(nu), dma(nu), dma(1), dma(1),
             ],
             compiler_params=pltpu.CompilerParams(collective_id=1, has_side_effects=True, vmem_limit_bytes=67043328),
             name='mlp',

time: 175 us -> 162 us (0.926)
  Pallas kernels: 164 us -> 154 us
  local copies, waits for them, and re-layouts: 8.36 us -> 4.22 us
  other arithmetic: 0.51 us -> 2.39 us
    pallas_call x1, Pallas kernels: 66.1 us -> 59.1 us  [device_layer(): pl.pallas_call(mlp_kernel, out_shape=jax.ShapeDtypeStruct((shard_rows, wi...]
    unnamed x13 -> x1, local copies, waits for them, and re-layouts: 7.04 us -> 1.59 us
    pallas_call x1, Pallas kernels: 98.3 us -> 95 us  [device_layer(): pl.pallas_call(attention_kernel, out_shape=(jax.ShapeDtypeStruct((chip_ro...]
where the time goes in v2:
time: 162 us; the launch traced here: 161 us
  Pallas kernels  154 us (95%)
  local copies, waits for them, and re-layouts  4.22 us (3%)
  other arithmetic  2.39 us (1%)
    pallas_call x1, Pallas kernels, device_layer(): pl.pallas_call(attention_kernel, out_shape=(jax.ShapeDtypeStruct((chip_ro...  95 us
    pallas_call x1, Pallas kernels, device_layer(): pl.pallas_call(mlp_kernel, out_shape=jax.ShapeDtypeStruct((shard_rows, wi...  59.1 us

profile of v2, /device:TPU:99, one launch (start us, length us, event | category | flops | bytes accessed | tf_op | source)
XLA Modules:
  0.0 161.4 jit_solution(9041678719004781732)
XLA Ops:
  0.7 0.3 fusion.29
  1.0 0.8 pad_maximum_fusion
  1.8 0.7 fusion.14.relk_ref
  2.4 1.3 reshape.512.gain
  3.8 0.6 fusion.30.relq_ref
  4.4 95.0 %attention.1 = (bf16[128,1024]{1,0:T(8,128)(2,1)}, bf16[32,2560]{1,0:T(8,128)(2,1)}) custom-call(bf16[16,5120]{1,0:T(8,128)(2,1)} %x_in.1, s32[1]{0:T(128)} %copy.15.len_ref, bf16[1024,1024]{1,0:T(8,128)(2,1)} %ck.1, bf16[1024,1024]{1,0:T(8,128)(2,1)} %cv.1, bf16[1,5120]{1,0:T(2,128)(2,1)} %reshape.512.gain, bf16[5120,1024]{1,0:T(8,128)(2,1)} %wq.1, ...), custom_call_target="tpu_custom_call" | custom-call | tf_op jit(solution)/shard_map/attention/pallas_call | solution.py:591
  99.4 1.3 reshape.513.gain
  100.7 59.1 %mlp.1 = bf16[16,5120]{1,0:T(8,128)(2,1)} custom-call(bf16[128,1024]{1,0:T(8,128)(2,1)} %get-tuple-element.7.o_in, bf16[32,2560]{1,0:T(8,128)(2,1)} %get-tuple-element.8.xres, bf16[2,2560]{1,0:T(2,128)(2,1)} %reshape.513.gain, bf16[1024,5120]{1,0:T(8,128)(2,1)} %wo.1, bf16[5120,3584]{1,0:T(8,128)(2,1)} %wg.1, bf16[5120,3584]{1,0:T(8,128)(2,1)} %wu.1, ...), custom_call_target="tpu_custom_call" | custom-call | tf_op jit(solution)/shard_map/mlp/pallas_call | solution.py:634
  159.8 1.6 copy.16
  (2 shorter events, 0.0 us)

commit v3 on v2

--- a/solution.py
+++ b/solution.py
@@ -111,7 +111,8 @@
         pltpu.make_async_copy(wk.at[:, pl.ds(pl.multiple_of(core * HEAD_DIM, HEAD_DIM), HEAD_DIM)], wkv, lsem.at[2]),
         pltpu.make_async_copy(wv.at[:, pl.ds(pl.multiple_of(core * HEAD_DIM, HEAD_DIM), HEAD_DIM)], wvv, lsem.at[3]),
     ]
-    for copy in local:
+    local[0].start()
+    for copy in local[1:]:
         copy.start()
 
     peers = [partner, me.mirrored(0), me.mirrored(1)]
@@ -239,12 +240,11 @@
     my_rows = q_rows(vx)
     vnew_t = qall[my_rows, head_w + HEAD_DIM:].T
     knew = qall[my_rows, head_w:head_w + HEAD_DIM]
-    relk = relk_ref[...]
 
     def new_head(h, carry):
         for j in range(tiles):
             s = lax.dot_general(knew, qaug[h, j * tile:(j + 1) * tile, 0:HEAD_DIM], contract_last, preferred_element_type=F32)
-            causal = jnp.broadcast_to(relk, s.shape) <= jnp.broadcast_to(relq_ref[:, j * tile:(j + 1) * tile], s.shape)
+            causal = jnp.broadcast_to(relk_ref[...], s.shape) <= jnp.broadcast_to(relq_ref[:, j * tile:(j + 1) * tile], s.shape)
             s = jnp.where(causal, s, -jnp.inf)
             finish(s, jnp.max(s, axis=0, keepdims=True), vnew_t, h, j, True, chip_rows)
         return carry
@@ -351,8 +351,8 @@
 
 
 def mlp_kernel(o_in, xres, gain, wo, wg, wu, wd, out,
-               wov, wgv, wuv, wdv, part, r1l, r1r, r2l, r2r, hbuf, hres, ubuf, fin, fbuf,
-               wosem, wgsem, wusem, wdsem, s1, q1, s2, q2, hs, hr, ps, pr, us, ur, fs, fr):
+               wgv, wuv, wdv, part, r1l, r1r, r2l, r2r, hbuf, hres, ubuf, fin, fbuf,
+               wsem, s1, q1, s2, q2, hs, hr, ps, pr, us, ur, fs, fr):
     me = Place()
     y, core = me.y, me.core
     nc, _, _, cw = part.shape
@@ -360,9 +360,9 @@
     width = 2 * half_w
     rows = o_in.shape[0]
     block_rows = rows // RING
-    nu, _, uw = wgv.shape
-    half_f = nu * uw
-    nd = wdv.shape[0]
+    half_f = wgv.shape[1]
+    uw = 256
+    nu = half_f // uw
     partner = me.at(core=1 - core)
     up, down = me.at(dy=1), me.at(dy=RING - 1)
     far, nxt, prev = (y + 2) % RING, (y + 1) % RING, (y + 3) % RING
@@ -371,25 +371,15 @@
     def lanes(start, size):
         return pl.ds(pl.multiple_of(start, 128), size)
 
-    def wo_copy(j):
-        return pltpu.make_async_copy(wo.at[:, lanes(col0 + j * cw, cw)], wov.at[j], wosem.at[j])
-
-    def wd_copy(j):
-        return pltpu.make_async_copy(wd.at[:, lanes(col0 + j * cw, cw)], wdv.at[j % nd], wdsem.at[j % nd])
-
-    def wg_copy(j):
-        return pltpu.make_async_copy(wg.at[:, lanes(core * half_f + j * uw, uw)], wgv.at[j], wgsem.at[j])
-
-    def wu_copy(j):
-        return pltpu.make_async_copy(wu.at[:, lanes(core * half_f + j * uw, uw)], wuv.at[j], wusem.at[j])
-
-    for j in range(nc):
-        wo_copy(j).start()
-    for j in range(nu):
-        wg_copy(j).start()
-        wu_copy(j).start()
-    for j in range(nd):
-        wd_copy(j).start()
+    wo_rows, wd_rows = wo.shape[0], wd.shape[0]
+    up_cols, out_cols = lanes(core * half_f, half_f), lanes(col0, half_w)
+    wo_load = pltpu.make_async_copy(wo.at[:, out_cols], wdv.at[pl.ds(0, wo_rows), :], wsem.at[0])
+    wd_load = pltpu.make_async_copy(wd.at[pl.ds(wo_rows, wd_rows - wo_rows), out_cols], wdv.at[pl.ds(wo_rows, wd_rows - wo_rows), :], wsem.at[1])
+    wd_late = pltpu.make_async_copy(wd.at[pl.ds(0, wo_rows), out_cols], wdv.at[pl.ds(0, wo_rows), :], wsem.at[2])
+    wg_load = pltpu.make_async_copy(wg.at[:, up_cols], wgv, wsem.at[3])
+    wu_load = pltpu.make_async_copy(wu.at[:, up_cols], wuv, wsem.at[4])
+    for copy in (wo_load, wg_load, wu_load, wd_load):
+        copy.start()
 
     barrier([up, down, partner])
 
@@ -424,15 +414,16 @@
         return carry
 
     attended = o_in[...]
+    wo_load.wait()
 
     def out_chunk(j, carry):
-        wo_copy(j).wait()
-        part[j] = jnp.dot(attended, wov[j], preferred_element_type=F32).reshape(RING, block_rows, cw)
+        part[j] = jnp.dot(attended, wdv[0:wo_rows, lanes(j * cw, cw)], preferred_element_type=F32).reshape(RING, block_rows, cw)
         for copy in first_sends(j):
             copy.start()
         return carry
 
     lax.fori_loop(0, nc, out_chunk, 0)
+    wd_late.start()
     lax.fori_loop(0, nc, relay, 0)
 
     def h_piece(c, p, j):
@@ -509,25 +500,28 @@
         return remote(at, at, us.at[j], ur.at[j], partner)
 
     def up_chunk(j, carry):
-        wg_copy(j).wait()
-        wu_copy(j).wait()
-        gate = jnp.dot(b0, wgv[j, 0:half_w, :], preferred_element_type=F32) + jnp.dot(b1, wgv[j, half_w:width, :], preferred_element_type=F32)
-        upper = jnp.dot(b0, wuv[j, 0:half_w, :], preferred_element_type=F32) + jnp.dot(b1, wuv[j, half_w:width, :], preferred_element_type=F32)
+        c = lanes(j * uw, uw)
+        gate = jnp.dot(b0, wgv[0:half_w, c], preferred_element_type=F32) + jnp.dot(b1, wgv[half_w:width, c], preferred_element_type=F32)
+        upper = jnp.dot(b0, wuv[0:half_w, c], preferred_element_type=F32) + jnp.dot(b1, wuv[half_w:width, c], preferred_element_type=F32)
         ubuf[:, lanes(core * half_f + j * uw, uw)] = (jax.nn.silu(gate) * upper).astype(BF16)
         u_copy(j, core).start()
         return carry
 
+    wg_load.wait()
+    wu_load.wait()
     lax.fori_loop(0, nu, up_chunk, 0)
+    wd_load.wait()
+    wd_late.wait()
     for j in range(nu):
         u_copy(j, 1 - core).wait_recv()
 
-    for j in range(nc):
-        wd_copy(j).wait()
-        part[j] = jnp.dot(ubuf[...], wdv[j % nd], preferred_element_type=F32).reshape(RING, block_rows, cw)
-        if j + nd < nc:
-            wd_copy(j + nd).start()
+    def down_chunk(j, carry):
+        part[j] = jnp.dot(ubuf[...], wdv[:, lanes(j * cw, cw)], preferred_element_type=F32).reshape(RING, block_rows, cw)
         for copy in first_sends(j):
             copy.start()
+        return carry
+
+    lax.fori_loop(0, nc, down_chunk, 0)
     lax.fori_loop(0, nc, relay, 0)
 
     def last_chunk(j, carry):
@@ -552,14 +546,11 @@
     return pltpu.SemaphoreType.DMA(shape)
 
 
-def relative_positions(chips, shards, row_count):
-    r = jnp.arange(row_count, dtype=jnp.int32)
-    per_chip = 2 * RING * 16
-    x = chips + r // per_chip
-    y, core, w = (r % per_chip) // 32, (r % 32) // 16, r % 16
+def relative_positions(r, shards):
+    x, y, core, w = r >> 7, (r >> 5) & 3, (r >> 4) & 1, r & 15
     k = (2 * x + core) * RING + y
     run = jnp.where(w < 8, k, 2 * shards - 1 - k)
-    return run * 8 + w % 8
+    return run * 8 + (w & 7)
 
 
 def solution(mesh):
@@ -576,16 +567,16 @@
         slots = cache_k.shape[0]
         head_w = w_query.shape[1] // 2
         heads = head_w // HEAD_DIM
+        half = HEAD_DIM // 2
         cp, y = lax.axis_index('cp'), lax.axis_index('tp')
-        half = HEAD_DIM // 2
-        own_rel = relative_positions(cp // 2, shards, chip_rows)
-        relk = relative_positions(jnp.where(cp % 2 == 0, cp // 2, y), shards, chip_rows)
-        relq = relative_positions(0, shards, rows)
-        inv_freq = 1.0 / (ROPE_BASE ** (jnp.arange(half, dtype=F32) * (2.0 / HEAD_DIM)))
-        angles = (cache_len[0] + own_rel).astype(F32)[:, None] * inv_freq[None, :]
-        cos, sin = jnp.cos(angles), jnp.sin(angles)
-        cos = jnp.concatenate([cos, cos], axis=1)
-        sin = jnp.concatenate([-sin, sin], axis=1)
+        ring_row = jnp.where(cp % 2 == 0, cp // 2, y)
+        relk = relative_positions(ring_row * chip_rows + lax.broadcasted_iota(jnp.int32, (chip_rows, 1), 0), shards)
+        relq = relative_positions(lax.broadcasted_iota(jnp.int32, (1, rows), 1), shards)
+        lane = jnp.arange(HEAD_DIM, dtype=jnp.int32)
+        rel = relative_positions((lax.axis_index('cp') // 2) * chip_rows + jnp.arange(chip_rows, dtype=jnp.int32), shards)
+        inv_freq = 1.0 / (ROPE_BASE ** ((lane % half).astype(F32) * (2.0 / HEAD_DIM)))
+        angles = (cache_len[0] + rel).astype(F32)[:, None] * inv_freq[None, :]
+        cos, sin = jnp.cos(angles), jnp.sin(angles) * jnp.where(lane < half, -1.0, 1.0)[None, :]
         block = (heads, HEAD_DIM + 8, chip_rows)
         part_block = (heads // 2,) + block[1:]
         attended, xres = pl.pallas_call(
@@ -622,14 +613,12 @@
             ],
             compiler_params=pltpu.CompilerParams(collective_id=0, has_side_effects=True, vmem_limit_bytes=67043328),
             name='attention',
-        )(hidden_loc, cache_len, cache_k, cache_v, norm1_gain.reshape(1, width), w_query, w_key, w_value, cos, sin, relq.reshape(1, rows), relk.reshape(chip_rows, 1))
+        )(hidden_loc, cache_len, cache_k, cache_v, norm1_gain.reshape(1, width), w_query, w_key, w_value, cos, sin, relq, relk)
 
         cw = 512 if half_w % 512 == 0 and half_w > 512 else 256
         nc = half_w // cw
         half_f = w_gate.shape[1] // 2
-        uw = 256
-        nu = half_f // uw
-        nd = max(1, nc - 1)
+        nu = half_f // 256
         br = 2 * shard_rows
         return pl.pallas_call(
             mlp_kernel,
@@ -637,10 +626,9 @@
             in_specs=[VMEM, VMEM, VMEM, ANY, ANY, ANY, ANY],
             out_specs=VMEM,
             scratch_shapes=[
-                pltpu.VMEM((nc, 2 * head_w, cw), BF16),
-                pltpu.VMEM((nu, width, uw), BF16),
-                pltpu.VMEM((nu, width, uw), BF16),
-                pltpu.VMEM((nd, 2 * half_f, cw), BF16),
+                pltpu.VMEM((width, half_f), BF16),
+                pltpu.VMEM((width, half_f), BF16),
+                pltpu.VMEM((2 * half_f, half_w), BF16),
                 pltpu.VMEM((nc, RING, br, cw), F32),
                 pltpu.VMEM((nc, br, cw // 2), F32),
                 pltpu.VMEM((nc, br, cw // 2), F32),
@@ -651,7 +639,7 @@
                 pltpu.VMEM((chip_rows, 2 * half_f), BF16),
                 pltpu.VMEM((2, shard_rows, half_w), BF16),
                 pltpu.VMEM((2, shard_rows, half_w), BF16),
-                dma(nc), dma(nu), dma(nu), dma(nd), dma(2, nc), dma(2, nc), dma(2, nc), dma(2, nc),
+                dma(5), dma(2, nc), dma(2, nc), dma(2, nc), dma(2, nc),
                 dma(4, nc), dma(4, nc), dma(4, nc), dma(4, nc), dma(nu), dma(nu), dma(1), dma(1),
             ],
             compiler_params=pltpu.CompilerParams(collective_id=1, has_side_effects=True, vmem_limit_bytes=67043328),

time: 162 us -> 152 us (0.938)
  Pallas kernels: 154 us -> 144 us
    pallas_call x1, Pallas kernels: 59.1 us -> 49.5 us  [device_layer(): pl.pallas_call(mlp_kernel, out_shape=jax.ShapeDtypeStruct((shard_rows, wi...]
where the time goes in v3:
time: 152 us
  Pallas kernels  144 us (95%)
  local copies, waits for them, and re-layouts  4.22 us (3%)
  other arithmetic  2.28 us (1%)
    pallas_call x1, Pallas kernels, device_layer(): pl.pallas_call(attention_kernel, out_shape=(jax.ShapeDtypeStruct((chip_ro...  95 us
    pallas_call x1, Pallas kernels, device_layer(): pl.pallas_call(mlp_kernel, out_shape=jax.ShapeDtypeStruct((shard_rows, wi...  49.5 us

profile of v3, /device:TPU:99, one launch (start us, length us, event | category | flops | bytes accessed | tf_op | source)
XLA Modules:
  0.0 151.6 jit_solution(12645701766128089525)
XLA Ops:
  0.0 0.7 fusion.2.relk_ref
  1.4 1.0 fusion
  2.3 1.3 reshape.198.gain
  3.6 0.6 fusion.6.relq_ref
  4.3 95.0 %attention.1 = (bf16[128,1024]{1,0:T(8,128)(2,1)}, bf16[32,2560]{1,0:T(8,128)(2,1)}) custom-call(bf16[16,5120]{1,0:T(8,128)(2,1)} %x_in.1, s32[1]{0:T(128)} %copy.16.len_ref, bf16[1024,1024]{1,0:T(8,128)(2,1)} %ck.1, bf16[1024,1024]{1,0:T(8,128)(2,1)} %cv.1, bf16[1,5120]{1,0:T(2,128)(2,1)} %reshape.198.gain, bf16[5120,1024]{1,0:T(8,128)(2,1)} %wq.1, ...), custom_call_target="tpu_custom_call" | custom-call | tf_op jit(solution)/shard_map/attention/pallas_call | solution.py:582
  99.3 1.3 reshape.199.gain
  100.6 49.5 %mlp.1 = bf16[16,5120]{1,0:T(8,128)(2,1)} custom-call(bf16[128,1024]{1,0:T(8,128)(2,1)} %get-tuple-element.7.o_in, bf16[32,2560]{1,0:T(8,128)(2,1)} %get-tuple-element.8.xres, bf16[2,2560]{1,0:T(2,128)(2,1)} %reshape.199.gain, bf16[1024,5120]{1,0:T(8,128)(2,1)} %wo.1, bf16[5120,3584]{1,0:T(8,128)(2,1)} %wg.1, bf16[5120,3584]{1,0:T(8,128)(2,1)} %wu.1, ...), custom_call_target="tpu_custom_call" | custom-call | tf_op jit(solution)/shard_map/mlp/pallas_call | solution.py:623
  150.0 1.6 %copy.17 = bf16[16,5120]{1,0:T(8,128)(2,1)} copy(bf16[16,5120]{1,0:T(8,128)(2,1)} %mlp.1) | data formatting | bytes 327680
  (2 shorter events, 0.0 us)
